TPU v7x, 128 devices: a whole 4x4x4 slice. The times are simulated.
128 devices in a mesh: ep: 64 (over y, x, z), dp: 2 (over core).
Axes of the slice: x: 4, y: 4, z: 4, core: 2. Of those that a mesh axis runs over, the one named last changes fastest.
Arguments:
- layer_input: bfloat16 [8192, 3584], P('ep'), may hold values from -6 to 6
- out_grad: bfloat16 [8192, 3584], P('ep'), may hold values from -6 to 6
- expert_ids: int32 [8192, 8], P('ep'), may hold values from 0 to 63, all different within a row; in each aligned block of 128 rows (0 to 127, 128 to 255, ...) at most 20 rows name the same one
- gate_probs: float32 [8192, 8], P('ep'), may hold values from 0.1 to 1
- gate_proj: bfloat16 [64, 3584, 1024], P('ep'), may hold values from -0.09375 to 0.09375
- up_proj: bfloat16 [64, 3584, 1024], P('ep'), may hold values from -0.09375 to 0.09375
- down_proj: bfloat16 [64, 1024, 3584], P('ep'), may hold values from -0.1875 to 0.1875
Outputs:
- input_grad: bfloat16 [8192, 3584], P('ep', 'dp')
Inputs may be any that keep to these rules, and one draw needn't show every extreme that they name: `expert_ids`: each row names 8 different experts. The 128 rows of one device name one expert at most 20 times, and in every draw some device's rows name some expert exactly 20 times.
All inputs are finite; a program needn't handle non-finite values.
Results may differ from a plain program's by a relative error of at most 0.0058.
Values may be sent and summed in bfloat16 or wider, within the bound.
No kernel may reach another device: no remote copies, remote signals or barrier semaphores. Data moves between devices by JAX's collectives and lax.ppermute only.
A program may use at most 192 MiB of HBM per device.

v0:
```python
import jax
import jax.numpy as jnp
from jax import lax
from jax.sharding import PartitionSpec as P


def split_up(shard, dim, size):
    shape = shard.shape
    parts = shard.reshape(*shape[:dim], size, shape[dim] // size, *shape[dim + 1 :])
    return jnp.moveaxis(parts, dim, 0)


def sum_at_owner(shard, axis, dim):
    parts = split_up(shard, dim, lax.axis_size(axis))
    arrived = lax.all_to_all(parts, axis, split_axis=0, concat_axis=0, tiled=True)
    return arrived.sum(axis=0)


def slot_ranks(flat_ids, experts_count):
    onehot = (flat_ids[:, None] == jnp.arange(experts_count, dtype=jnp.int32)[None, :]).astype(
        jnp.int32
    )
    running = jnp.cumsum(onehot, axis=0)
    return jnp.sum((running - 1) * onehot, axis=1)


def expert_backward(in_rows, grad_rows, gate_mat, up_mat, down_mat):
    gate_pre = jnp.dot(in_rows, gate_mat, preferred_element_type=jnp.float32)
    up_pre = jnp.dot(in_rows, up_mat, preferred_element_type=jnp.float32)
    hidden_grad = lax.dot_general(
        grad_rows, down_mat, (((1,), (1,)), ((), ())), preferred_element_type=jnp.float32
    )
    sigmoid = jax.nn.sigmoid(gate_pre)
    gate_grad = (hidden_grad * up_pre * sigmoid * (1.0 + gate_pre * (1.0 - sigmoid))).astype(
        jnp.bfloat16
    )
    up_grad = (hidden_grad * gate_pre * sigmoid).astype(jnp.bfloat16)
    back_gate = lax.dot_general(
        gate_grad, gate_mat, (((1,), (1,)), ((), ())), preferred_element_type=jnp.float32
    )
    back_up = lax.dot_general(
        up_grad, up_mat, (((1,), (1,)), ((), ())), preferred_element_type=jnp.float32
    )
    return back_gate + back_up


def body(layer_input, out_grad, expert_ids, gate_probs, gate_proj, up_proj, down_proj):
    experts_count = lax.axis_size("ep")
    tok_rows, features = layer_input.shape
    top_count = expert_ids.shape[1]
    capacity = 2 * ((5 * tok_rows * top_count + 8 * experts_count - 1) // (8 * experts_count))
    flat_ids = expert_ids.reshape(-1)
    route_count = flat_ids.shape[0]
    slot_rank = slot_ranks(flat_ids, experts_count)
    core_index = lax.axis_index("dp")
    span = capacity // 2
    local_rank = slot_rank - core_index * span
    inside = (local_rank >= 0) & (local_rank < span)
    slot_index = flat_ids * span + jnp.clip(local_rank, 0, span - 1)
    gate_mat, up_mat, down_mat = (gate_proj[0], up_proj[0], down_proj[0])
    route_weight = jnp.where(inside, gate_probs.reshape(-1), 0.0)
    target = jnp.where(inside, slot_index, experts_count * span)
    route_token = jnp.arange(route_count, dtype=jnp.int32) // top_count
    slot_token = (
        jnp.full((experts_count * span,), tok_rows, jnp.int32)
        .at[target]
        .set(route_token, mode="drop")
    )
    padded_in = jnp.concatenate([layer_input, jnp.zeros((1, features), layer_input.dtype)], 0)
    padded_grad = jnp.concatenate([out_grad, jnp.zeros((1, features), out_grad.dtype)], 0)
    in_buffer = jnp.take(padded_in, slot_token, axis=0).reshape(experts_count, span, features)
    grad_buffer = jnp.take(padded_grad, slot_token, axis=0).reshape(experts_count, span, features)
    in_rows = lax.all_to_all(in_buffer, "ep", split_axis=0, concat_axis=0, tiled=True)
    grad_rows = lax.all_to_all(grad_buffer, "ep", split_axis=0, concat_axis=0, tiled=True)
    sources = in_rows.shape[0]
    items = in_rows.shape[1]
    partial_value = expert_backward(
        in_rows.reshape(-1, features), grad_rows.reshape(-1, features), gate_mat, up_mat, down_mat
    )
    partial_value = partial_value.reshape(sources, items, features)
    returned = lax.all_to_all(
        partial_value.astype(jnp.bfloat16), "ep", split_axis=0, concat_axis=0, tiled=True
    )
    slot_rows = returned.reshape(experts_count * span, returned.shape[2])
    picked = jnp.take(slot_rows, slot_index, axis=0).astype(jnp.float32) * route_weight[:, None]
    summed = picked.reshape(tok_rows, top_count, slot_rows.shape[1]).sum(axis=1)
    summed = sum_at_owner(summed, "dp", 1)
    return summed.astype(jnp.bfloat16)


def solution(mesh):
    placed = (
        P("ep", None),
        P("ep", None),
        P("ep", None),
        P("ep", None),
        P("ep", None, None),
        P("ep", None, None),
        P("ep", None, None),
    )
    return jax.shard_map(body, mesh=mesh, in_specs=placed, out_specs=P("ep", "dp"), check_vma=False)
```

profile of v0, /device:TPU:1, one launch (start us, length us, event | category | flops | bytes accessed | tf_op | source)
XLA Modules:
  0.0 486.4 jit_solution(16474804561744417502)
XLA Ops:
  0.0 0.0 copy-start
  0.0 0.8 broadcast_multiply_fusion
  0.8 0.8 copy.37
  1.6 0.1 eq.26
  1.7 0.1 reshape.157
  1.8 18.0 %reduce-window.6 = s32[64,8,128]{2,1,0:T(8,128)S(1)} reduce-window(s32[64,8,128]{2,1,0:T(8,128)S(1)} %fusion.20, s32[]{:T(128)} %constant.35.clone.1), window={size=1x1x128 pad=0_0x0_0x127_0}, to_apply=%region_0.0 | reduce-window | flops 8323072 | bytes 524292 | tf_op jit(solution)/shard_map/reduce-window
  19.8 0.1 slice.14
  19.9 0.1 copy.39
  20.1 0.1 copy.40
  20.2 0.1 add_add_fusion
  20.3 0.1 fusion.19
  20.4 0.1 copy.43
  20.5 0.1 mul.56
  20.7 4.3 scatter_custom_fusion
  25.0 1.2 concatenate.7
  26.3 0.0 copy-done
  26.3 0.1 concatenate.6
  26.4 5.1 %gather_fusion.1 = bf16[640,3584]{1,0:T(8,128)(2,1)} fusion(bf16[129,3584]{1,0:T(8,128)(2,1)S(1)} %concatenate.6, s32[1024]{0:T(1024)S(1)} %pad_clamp_fusion), kind=kCustom, calls=%fused_computation.clone | custom fusion | bytes 9177600 | tf_op jit(solution)/shard_map/jit(_take)/gather | solution.py:72
  31.5 5.2 %gather_fusion.2 = bf16[640,3584]{1,0:T(8,128)(2,1)} fusion(bf16[129,3584]{1,0:T(8,128)(2,1)S(1)} %concatenate.7, s32[1024]{0:T(1024)S(1)} %pad_clamp_fusion), kind=kCustom, calls=%fused_computation.1.clone | custom fusion | bytes 9177600 | tf_op jit(solution)/shard_map/jit(_take)/gather | solution.py:71
  36.6 8.1 %broadcast_select_fusion.1 = (bf16[640,3584]{1,0:T(8,128)(2,1)}, bf16[640,3584]{1,0:T(8,128)(2,1)}) fusion(bf16[640,3584]{1,0:T(8,128)(2,1)} %gather_fusion.1, pred[640]{0:T(1024)(128)(4,1)S(1)} %compare_and_fusion, bf16[640,3584]{1,0:T(8,128)(2,1)} %gather_fusion.2), kind=kLoop, calls=%fused_computation.18 | loop fusion | flops 4587520 | bytes 18350720 | tf_op jit(solution)/shard_map/jit(_take)/select_n | solution.py:72
  44.7 7.7 %reshape.159 = bf16[64,10,3584]{2,1,0:T(8,128)(2,1)} reshape(bf16[640,3584]{1,0:T(8,128)(2,1)} %get-tuple-element.8) | data formatting | bytes 9175040 | tf_op jit(solution)/shard_map/reshape | solution.py:72
  52.4 12.2 %all-to-all-start = ((bf16[64,10,3584]{2,1,0:T(8,128)(2,1)}), bf16[64,10,3584]{2,1,0:T(8,128)(2,1)}, u32[]{:S(2)}, u32[]{:S(2)}) async-start(bf16[64,10,3584]{2,1,0:T(8,128)(2,1)} %reshape.159), calls=%async_computation | async-start | bytes 14680064 | tf_op jit(solution)/shard_map/all_to_all | solution.py:74
  64.6 7.7 %reshape.161 = bf16[64,10,3584]{2,1,0:T(8,128)(2,1)} reshape(bf16[640,3584]{1,0:T(8,128)(2,1)} %get-tuple-element.9) | data formatting | bytes 9175040 | tf_op jit(solution)/shard_map/reshape | solution.py:71
  72.3 85.3 %all-to-all-done = bf16[64,10,3584]{2,1,0:T(8,128)(2,1)} async-done(((bf16[64,10,3584]{2,1,0:T(8,128)(2,1)}), bf16[64,10,3584]{2,1,0:T(8,128)(2,1)}, u32[]{:S(2)}, u32[]{:S(2)}) %all-to-all-start) | async-done | bytes 4587552 | tf_op jit(solution)/shard_map/all_to_all | solution.py:74
  157.6 11.7 %all-to-all-start.1 = ((bf16[64,10,3584]{2,1,0:T(8,128)(2,1)}), bf16[64,10,3584]{2,1,0:T(8,128)(2,1)}, u32[]{:S(2)}, u32[]{:S(2)}) async-start(bf16[64,10,3584]{2,1,0:T(8,128)(2,1)} %reshape.161), calls=%async_computation.1 | async-start | bytes 14680064 | tf_op jit(solution)/shard_map/all_to_all | solution.py:73
  169.3 7.9 %reshape.160 = bf16[640,3584]{1,0:T(8,128)(2,1)} reshape(bf16[64,10,3584]{2,1,0:T(8,128)(2,1)} %all-to-all-done) | data formatting | bytes 9175040 | tf_op jit(solution)/shard_map/reshape | solution.py:78
  177.2 8.6 %fusion.8 = f32[640,1024]{1,0:T(8,128)S(1)} fusion(bf16[640,3584]{1,0:T(8,128)(2,1)} %reshape.160, bf16[1,1024,3584]{2,1,0:T(8,128)(2,1)} %param.15), kind=kOutput, calls=%fused_computation.15 | convolution fusion | flops 4697620480 | bytes 14548992 | tf_op jit(solution)/shard_map/dot_general | solution.py:30
  185.8 84.1 %all-to-all-done.1 = bf16[64,10,3584]{2,1,0:T(8,128)(2,1)} async-done(((bf16[64,10,3584]{2,1,0:T(8,128)(2,1)}), bf16[64,10,3584]{2,1,0:T(8,128)(2,1)}, u32[]{:S(2)}, u32[]{:S(2)}) %all-to-all-start.1) | async-done | bytes 4587552 | tf_op jit(solution)/shard_map/all_to_all | solution.py:73
  269.9 8.0 %reshape.162 = bf16[640,3584]{1,0:T(8,128)(2,1)} reshape(bf16[64,10,3584]{2,1,0:T(8,128)(2,1)} %all-to-all-done.1) | data formatting | bytes 9175040 | tf_op jit(solution)/shard_map/reshape | solution.py:78
  277.9 10.9 %fusion.2 = f32[640,1024]{1,0:T(8,128)} fusion(bf16[640,3584]{1,0:T(8,128)(2,1)} %reshape.162, bf16[1,3584,1024]{2,1,0:T(8,128)(2,1)} %param.13), kind=kOutput, calls=%fused_computation.9 | convolution fusion | flops 4697620480 | bytes 14548992 | tf_op jit(solution)/shard_map/dot_general | solution.py:28
  288.8 18.6 %fusion = f32[640,3584]{1,0:T(8,128)} fusion(bf16[1,3584,1024]{2,1,0:T(8,128)(2,1)} %param.13, f32[640,1024]{1,0:T(8,128)} %fusion.2, f32[640,1024]{1,0:T(8,128)S(1)} %fusion.8, bf16[640,3584]{1,0:T(8,128)(2,1)} %reshape.162, bf16[1,3584,1024]{2,1,0:T(8,128)(2,1)} %param.14), kind=kOutput, calls=%fused_computation.7 | convolution fusion | flops 9401794560 | bytes 33685504 | tf_op jit(solution)/shard_map/dot_general | solution.py:38
  307.4 13.5 %add_convert_fusion = bf16[640,3584]{1,0:T(8,128)(2,1)} fusion(f32[640,3584]{1,0:T(8,128)} %fusion, bf16[1,3584,1024]{2,1,0:T(8,128)(2,1)} %param.14, f32[640,1024]{1,0:T(8,128)S(1)} %fusion.8, f32[640,1024]{1,0:T(8,128)} %fusion.2), kind=kOutput, calls=%fused_computation.5 | convolution fusion | flops 4706140160 | bytes 26345472 | tf_op jit(solution)/shard_map/dot_general | solution.py:41
  320.9 7.7 %convert_element_type.28 = bf16[64,10,3584]{2,1,0:T(8,128)(2,1)} reshape(bf16[640,3584]{1,0:T(8,128)(2,1)} %add_convert_fusion) | data formatting | bytes 9175040 | tf_op jit(solution)/shard_map/convert_element_type | solution.py:82
  328.6 11.4 %all-to-all-start.2 = ((bf16[64,10,3584]{2,1,0:T(8,128)(2,1)}), bf16[64,10,3584]{2,1,0:T(8,128)(2,1)}, u32[]{:S(2)}, u32[]{:S(2)}) async-start(bf16[64,10,3584]{2,1,0:T(8,128)(2,1)} %convert_element_type.28), calls=%async_computation.2 | async-start | bytes 14680064 | tf_op jit(solution)/shard_map/all_to_all | solution.py:81
  340.0 0.1 and.41
  340.1 0.1 min.14
  340.2 0.0 copy-done.2
  340.2 0.1 copy.44
  340.4 0.0 copy-done.1
  340.4 0.1 copy.42
  340.5 93.0 %all-to-all-done.2 = bf16[64,10,3584]{2,1,0:T(8,128)(2,1)} async-done(((bf16[64,10,3584]{2,1,0:T(8,128)(2,1)}), bf16[64,10,3584]{2,1,0:T(8,128)(2,1)}, u32[]{:S(2)}, u32[]{:S(2)}) %all-to-all-start.2) | async-done | bytes 4587552 | tf_op jit(solution)/shard_map/all_to_all | solution.py:81
  433.6 8.0 %reshape.163 = bf16[640,3584]{1,0:T(8,128)(2,1)} reshape(bf16[64,10,3584]{2,1,0:T(8,128)(2,1)} %all-to-all-done.2) | data formatting | bytes 9175040 | tf_op jit(solution)/shard_map/reshape | solution.py:84
  441.6 16.7 %gather_fusion = bf16[1024,3584]{1,0:T(8,128)(2,1)} fusion(bf16[640,3584]{1,0:T(8,128)(2,1)} %reshape.163, s32[1024]{0:T(1024)S(1)} %broadcast_clamp_fusion), kind=kCustom, calls=%fused_computation.2 | custom fusion | bytes 14684160 | tf_op jit(solution)/shard_map/jit(_take)/gather | solution.py:85
  458.3 13.6 %multiply_reduce_fusion = f32[128,3584]{1,0:T(8,128)} fusion(bf16[1024,3584]{1,0:T(8,128)(2,1)} %gather_fusion, f32[128,8]{1,0:T(8,128)S(1)} %broadcast_select_fusion.2, pred[128,8]{1,0:T(8,128)(4,1)S(1)} %copy.42), kind=kLoop, calls=%fused_computation.4 | loop fusion | flops 14221312 | bytes 9180160 | tf_op jit(solution)/shard_map/reduce_sum | solution.py:86
  471.9 1.8 copy.45
  473.7 1.7 copy.46
  475.4 9.9 %all_to_all.20 = f32[2,128,1792]{2,1,0:T(8,128)S(1)} all-to-all(f32[2,128,1792]{2,1,0:T(8,128)} %copy.46), channel_id=1, replica_groups=mesh['ep'=64,'dp'=2] {'dp'}, dimensions={0} | all-to-all | bytes 3670016 | tf_op jit(solution)/shard_map/all_to_all | solution.py:15
  485.4 1.0 reduce_sum.29
  (16 shorter events, 0.2 us)
Async XLA Ops:
  0.0 26.3 %copy-start = (bf16[128,3584]{1,0:T(8,128)(2,1)S(1)}, bf16[128,3584]{1,0:T(8,128)(2,1)}, u32[]{:S(2)}) copy-start(bf16[128,3584]{1,0:T(8,128)(2,1)} %param.10) | copy-start | bytes 2752516
  52.4 105.2 %all-to-all-start = ((bf16[64,10,3584]{2,1,0:T(8,128)(2,1)}), bf16[64,10,3584]{2,1,0:T(8,128)(2,1)}, u32[]{:S(2)}, u32[]{:S(2)}) async-start(bf16[64,10,3584]{2,1,0:T(8,128)(2,1)} %reshape.159), calls=%async_computation | async-start | bytes 14680064 | tf_op jit(solution)/shard_map/all_to_all | solution.py:74
  157.6 112.3 %all-to-all-start.1 = ((bf16[64,10,3584]{2,1,0:T(8,128)(2,1)}), bf16[64,10,3584]{2,1,0:T(8,128)(2,1)}, u32[]{:S(2)}, u32[]{:S(2)}) async-start(bf16[64,10,3584]{2,1,0:T(8,128)(2,1)} %reshape.161), calls=%async_computation.1 | async-start | bytes 14680064 | tf_op jit(solution)/shard_map/all_to_all | solution.py:73
  328.6 11.6 %copy-start.2 = (f32[128,8]{0,1:T(8,128)S(1)}, f32[128,8]{0,1:T(8,128)}, u32[]{:S(2)}) copy-start(f32[128,8]{0,1:T(8,128)} %param.12) | copy-start | bytes 12292
  328.6 11.8 %copy-start.1 = (s32[128,8]{0,1:T(8,128)S(1)}, s32[128,8]{0,1:T(8,128)}, u32[]{:S(2)}) copy-start(s32[128,8]{0,1:T(8,128)} %param.11) | copy-start | bytes 12292
  328.6 105.0 %all-to-all-start.2 = ((bf16[64,10,3584]{2,1,0:T(8,128)(2,1)}), bf16[64,10,3584]{2,1,0:T(8,128)(2,1)}, u32[]{:S(2)}, u32[]{:S(2)}) async-start(bf16[64,10,3584]{2,1,0:T(8,128)(2,1)} %convert_element_type.28), calls=%async_computation.2 | async-start | bytes 14680064 | tf_op jit(solution)/shard_map/all_to_all | solution.py:81
where the time goes:
time: 494 us; the launch traced here: 486 us
  waiting for transfers between devices  262 us (53%)
  local copies, waits for them, and re-layouts  85.1 us (17%)
  matrix products  51.5 us (10%)
  other arithmetic  41.8 us (8%)
  starting transfers between devices  35.3 us (7%)
  blocking collectives  9.92 us (2%)
    all_to_all x1, waiting for transfers between devices, body(): lax.all_to_all(partial_value.astype(jnp.bfloat16), 'ep', split_axis=0, co...  93 us
    all_to_all x1, waiting for transfers between devices, body(): lax.all_to_all(grad_buffer, 'ep', split_axis=0, concat_axis=0, tiled=True)  85.3 us
    all_to_all x1, waiting for transfers between devices, body(): lax.all_to_all(in_buffer, 'ep', split_axis=0, concat_axis=0, tiled=True)  84.1 us
    dot_general x1, matrix products, expert_backward(): lax.dot_general(gate_grad, gate_mat, (((1,), (1,)), ((), ())), preferred_...  18.6 us
    another operation x2, other arithmetic  18 us
    gather x1, local copies, waits for them, and re-layouts, body(): jnp.take(slot_rows, slot_index, axis=0).astype(jnp.float32)  16.7 us
    reduce_sum x1, other arithmetic, body(): summed = picked.reshape(tok_rows, top_count, slot_rows.shape[1]).sum(axis=1)  13.6 us
    dot_general x1, matrix products, expert_backward(): lax.dot_general(up_grad, up_mat, (((1,), (1,)), ((), ())), preferred_elem...  13.5 us
  transfers between devices with their start and end apart: 3, of which 3 were waited for; matrix products, arithmetic and copies ran while one was open for 5% of the time, Pallas kernels for 0%

commit v1 on v0

v1 whole, which is shorter than its diff:
```python
import jax
import jax.numpy as jnp
from jax import lax
from jax.experimental import pallas as pl
from jax.experimental.pallas import tpu as pltpu
from jax.sharding import PartitionSpec as P

BF16, F32 = jnp.bfloat16, jnp.float32
TILE = 8
WIDE, TAIL = 512, 128
STEP = WIDE + TAIL
FOLD = WIDE // TAIL


def iota(shape, dim):
    return lax.broadcasted_iota(jnp.int32, shape, dim)


def slot_keys(ids_ref, base, experts):
    top, tokens = ids_ref.shape
    number = iota((experts, tokens), 0)
    named = ids_ref[0:1, :] == number
    for k in range(1, top):
        named = named | (ids_ref[k : k + 1, :] == number)
    before = jnp.where(iota((tokens, tokens), 0) < iota((tokens, tokens), 1), 1.0, 0.0).astype(BF16)
    rank = jnp.dot(jnp.where(named, 1.0, 0.0).astype(BF16), before, preferred_element_type=F32)
    key = jnp.where(named, rank - base, -100.0).astype(BF16)
    return jnp.dot(spread(experts), key, preferred_element_type=F32)


def spread(experts):
    shape = (experts * TILE, experts)
    return jnp.where(iota(shape, 0) // TILE == iota(shape, 1), 1.0, 0.0).astype(BF16)


def dispatch_kernel(experts, base_ref, ids_ref, x_ref, g_ref, out_ref, main_sel, tail_sel):
    step, half = pl.program_id(0), pl.num_programs(0) // 2
    tokens = ids_ref.shape[1]

    @pl.when(step == 0)
    def _():
        key = slot_keys(ids_ref, base_ref[0].astype(F32), experts)
        row = iota(key.shape, 0) % TILE
        main_sel[...] = jnp.where(key == row.astype(F32), 1.0, 0.0).astype(BF16)
        late = key == (TILE + row % 2).astype(F32)
        for q in range(FOLD):
            tail_sel[:, q * tokens : (q + 1) * tokens] = jnp.where(late & (row // 2 == q), 1.0, 0.0).astype(BF16)

    def put(ref):
        block = ref[...]
        out_ref[:, 0:WIDE] = jnp.dot(main_sel[...], block, preferred_element_type=F32).astype(BF16)
        parts = jnp.concatenate([block[:, q * TAIL : (q + 1) * TAIL] for q in range(FOLD)], 0)
        out_ref[:, WIDE:STEP] = jnp.dot(tail_sel[...], parts, preferred_element_type=F32).astype(BF16)

    @pl.when(step < half)
    def _():
        put(x_ref)

    @pl.when(step >= half)
    def _():
        put(g_ref)


def dispatch(base, ids, x, g, experts):
    tokens, features = x.shape
    blocks = features // WIDE
    rows = experts * TILE
    return pl.pallas_call(
        lambda *refs: dispatch_kernel(experts, *refs),
        grid=(2 * blocks,),
        in_specs=[
            pl.BlockSpec(memory_space=pltpu.SMEM),
            pl.BlockSpec(ids.shape, lambda s: (0, 0)),
            pl.BlockSpec((tokens, WIDE), lambda s: (0, jnp.minimum(s, blocks - 1))),
            pl.BlockSpec((tokens, WIDE), lambda s: (0, jnp.maximum(s - blocks, 0))),
        ],
        out_specs=pl.BlockSpec((rows, STEP), lambda s: (0, s)),
        out_shape=jax.ShapeDtypeStruct((rows, 2 * blocks * STEP), BF16),
        scratch_shapes=[pltpu.VMEM((rows, tokens), BF16), pltpu.VMEM((rows, FOLD * tokens), BF16)],
        name="dispatch",
    )(base, ids, x, g)


def weights_kernel(experts, base_ref, ids_ref, probs_ref, main_ref, tail_ref):
    top, tokens = ids_ref.shape
    key = slot_keys(ids_ref, base_ref[0].astype(F32), experts)
    number = iota((experts, tokens), 0)
    prob = jnp.zeros((experts, tokens), F32)
    for k in range(top):
        prob = prob + jnp.where(ids_ref[k : k + 1, :] == number, probs_ref[k : k + 1, :], 0.0)
    high = prob.astype(BF16)
    low = (prob - high.astype(F32)).astype(BF16)
    row = iota(key.shape, 0) % TILE
    main, late = key == row.astype(F32), key == (TILE + row % 2).astype(F32)
    for n, part in enumerate((high, low)):
        wide = jnp.dot(spread(experts), part, preferred_element_type=F32)
        main_ref[n * tokens : (n + 1) * tokens, :] = jnp.where(main, wide, 0.0).T.astype(BF16)
        for q in range(FOLD):
            at = (2 * q + n) * tokens
            tail_ref[at : at + tokens, :] = jnp.where(late & (row // 2 == q), wide, 0.0).T.astype(BF16)


def combine_weights(base, ids, probs, experts):
    tokens = ids.shape[1]
    rows = experts * TILE
    return pl.pallas_call(
        lambda *refs: weights_kernel(experts, *refs),
        in_specs=[
            pl.BlockSpec(memory_space=pltpu.SMEM),
            pl.BlockSpec(memory_space=pltpu.VMEM),
            pl.BlockSpec(memory_space=pltpu.VMEM),
        ],
        out_shape=[
            jax.ShapeDtypeStruct((2 * tokens, rows), BF16),
            jax.ShapeDtypeStruct((2 * FOLD * tokens, rows), BF16),
        ],
        name="combine_weights",
    )(base, ids, probs)


def unfold_matrix(rows, transposed):
    sources = rows // TILE
    unfolded, packed = iota((rows, rows), int(transposed)), iota((rows, rows), 1 - int(transposed))
    per = 2 * sources
    q, rest = unfolded // per, unfolded % per
    at = (rest // 2) * TILE + 2 * q + rest % 2
    return jnp.where(at == packed, 1.0, 0.0).astype(BF16)


def expert_kernel(chunks, packet_ref, gate_cols, up_cols, down_rows, gate_rows, up_rows, out_ref, x_s, g_s, tail_s, gg_s, ug_s, fold_s, sems):
    step = pl.program_id(0)
    rows = packet_ref.shape[0]
    late = rows // FOLD
    blocks = x_s.shape[1] // WIDE

    @pl.when(step == 0)
    def _():
        copies = []
        for n, dst in enumerate((x_s, g_s)):
            for j in range(blocks):
                at = (n * blocks + j) * STEP
                copies.append(pltpu.make_async_copy(packet_ref.at[:, at : at + WIDE], dst.at[0:rows, j * WIDE : (j + 1) * WIDE], sems.at[n]))
                copies.append(pltpu.make_async_copy(packet_ref.at[:, at + WIDE : at + STEP], tail_s.at[n, :, j * TAIL : (j + 1) * TAIL], sems.at[n]))
        for copy in copies:
            copy.start()
        unfold = unfold_matrix(rows, False)
        fold_s[...] = unfold_matrix(rows, True)
        for n, dst in enumerate((x_s, g_s)):
            for copy in copies[n * 2 * blocks : (n + 1) * 2 * blocks]:
                copy.wait()
            tail = jnp.dot(unfold, tail_s[n], preferred_element_type=F32).astype(BF16)
            for q in range(FOLD):
                for j in range(blocks):
                    dst[rows : rows + late, j * WIDE + q * TAIL : j * WIDE + (q + 1) * TAIL] = tail[q * late : (q + 1) * late, j * TAIL : (j + 1) * TAIL]

    @pl.when(step < chunks)
    def _():
        gate_pre = jnp.dot(x_s[...], gate_cols[...], preferred_element_type=F32)
        up_pre = jnp.dot(x_s[...], up_cols[...], preferred_element_type=F32)
        hidden_grad = lax.dot_general(g_s[...], down_rows[...], (((1,), (1,)), ((), ())), preferred_element_type=F32)
        sigmoid = jax.nn.sigmoid(gate_pre)
        common = hidden_grad * sigmoid
        gg_s[step] = (common * up_pre * (1.0 + gate_pre * (1.0 - sigmoid))).astype(BF16)
        ug_s[step] = (common * gate_pre).astype(BF16)

    @pl.when(step >= chunks)
    def _():
        width = gg_s.shape[2]
        gg = jnp.concatenate([gg_s[c] for c in range(chunks)], 1)
        ug = jnp.concatenate([ug_s[c] for c in range(chunks)], 1)
        back = lax.dot_general(gg, gate_rows[...], (((1,), (1,)), ((), ())), preferred_element_type=F32)
        back = back + lax.dot_general(ug, up_rows[...], (((1,), (1,)), ((), ())), preferred_element_type=F32)
        back = back.astype(BF16)
        out_ref[:, 0:WIDE] = back[0:rows]
        parts = jnp.concatenate([back[rows:, q * TAIL : (q + 1) * TAIL] for q in range(FOLD)], 0)
        out_ref[:, WIDE:STEP] = jnp.dot(fold_s[...], parts, preferred_element_type=F32).astype(BF16)


def expert_backward(packets, gate, up, down):
    features, hidden = gate.shape
    rows = packets.shape[0]
    items = rows + rows // FOLD
    blocks = features // WIDE
    width = 256
    chunks = hidden // width
    first = lambda s: jnp.minimum(s, chunks - 1)
    second = lambda s: jnp.maximum(s - chunks, 0)
    return pl.pallas_call(
        lambda *refs: expert_kernel(chunks, *refs),
        grid=(chunks + blocks,),
        in_specs=[
            pl.BlockSpec(memory_space=pl.ANY),
            pl.BlockSpec((features, width), lambda s: (0, first(s))),
            pl.BlockSpec((features, width), lambda s: (0, first(s))),
            pl.BlockSpec((width, features), lambda s: (first(s), 0)),
            pl.BlockSpec((WIDE, hidden), lambda s: (second(s), 0)),
            pl.BlockSpec((WIDE, hidden), lambda s: (second(s), 0)),
        ],
        out_specs=pl.BlockSpec((rows, STEP), lambda s: (0, second(s))),
        out_shape=jax.ShapeDtypeStruct((rows, blocks * STEP), BF16),
        scratch_shapes=[
            pltpu.VMEM((items, features), BF16),
            pltpu.VMEM((items, features), BF16),
            pltpu.VMEM((2, rows, blocks * TAIL), BF16),
            pltpu.VMEM((chunks, items, width), BF16),
            pltpu.VMEM((chunks, items, width), BF16),
            pltpu.VMEM((rows, rows), BF16),
            pltpu.SemaphoreType.DMA((2,)),
        ],
        compiler_params=pltpu.CompilerParams(vmem_limit_bytes=60 * 1024 * 1024),
        name="expert_backward",
    )(packets, gate, up, down, gate, up)


def combine_kernel(main_ref, tail_ref, back_ref, out_ref):
    tokens = out_ref.shape[0]
    both = jnp.dot(main_ref[...], back_ref[:, 0:WIDE], preferred_element_type=F32)
    late = jnp.dot(tail_ref[...], back_ref[:, WIDE:STEP], preferred_element_type=F32)
    for q in range(FOLD):
        cols = slice(q * TAIL, (q + 1) * TAIL)
        at = 2 * q * tokens
        low = both[tokens:, cols] + late[at + tokens : at + 2 * tokens]
        out_ref[:, cols] = both[:tokens, cols] + late[at : at + tokens] + low


def combine(main, tail, back):
    rows, width = back.shape
    blocks = width // STEP
    tokens = main.shape[0] // 2
    return pl.pallas_call(
        combine_kernel,
        grid=(blocks,),
        in_specs=[
            pl.BlockSpec(main.shape, lambda s: (0, 0)),
            pl.BlockSpec(tail.shape, lambda s: (0, 0)),
            pl.BlockSpec((rows, STEP), lambda s: (0, s)),
        ],
        out_specs=pl.BlockSpec((tokens, WIDE), lambda s: (0, s)),
        out_shape=jax.ShapeDtypeStruct((tokens, blocks * WIDE), F32),
        name="combine",
    )(main, tail, back)


def exchange(packets, experts):
    parts = packets.reshape(experts, TILE, -1)
    return lax.all_to_all(parts, "ep", split_axis=0, concat_axis=0, tiled=True).reshape(packets.shape)


def body(layer_input, out_grad, expert_ids, gate_probs, gate_proj, up_proj, down_proj):
    experts = lax.axis_size("ep")
    core = lax.axis_index("dp")
    features = layer_input.shape[1]
    ids = expert_ids.T
    base = jnp.full((1,), (TILE + 2) * core, jnp.int32)
    packets = dispatch(base, ids, layer_input, out_grad, experts)
    arrived = exchange(packets, experts)
    main, tail = combine_weights(base, ids, gate_probs.T, experts)
    back = expert_backward(arrived, gate_proj[0], up_proj[0], down_proj[0])
    returned = exchange(back, experts)
    summed = combine(main, tail, returned)
    half = features // 2
    other = lax.dynamic_slice_in_dim(summed, (1 - core) * half, half, 1)
    own = lax.dynamic_slice_in_dim(summed, core * half, half, 1)
    return (own + lax.ppermute(other, "dp", ((0, 1), (1, 0)))).astype(BF16)


def solution(mesh):
    rows = P("ep", None)
    mats = P("ep", None, None)
    return jax.shard_map(body, mesh=mesh, in_specs=(rows,) * 4 + (mats,) * 3, out_specs=P("ep", "dp"), check_vma=False)
```

time: 494 us -> 252 us (0.51)
  waiting for transfers between devices: 262 us -> 56.4 us
  blocking collectives: 9.92 us -> 117 us
  local copies, waits for them, and re-layouts: 85.1 us -> 1.24 us
  Pallas kernels: 0 us -> 62.5 us
  matrix products: 51.5 us -> 0 us
  other arithmetic: 41.8 us -> 2.03 us
  starting transfers between devices: 35.3 us -> 8.71 us
    all_to_all x3 -> x1, waiting for transfers between devices: 262 us -> 54.3 us  [exchange(): lax.all_to_all(parts, 'ep', split_axis=0, concat_axis=0, tiled=True)]
    all_to_all x1, blocking collectives: 9.92 us -> 117 us  [exchange(): lax.all_to_all(parts, 'ep', split_axis=0, concat_axis=0, tiled=True)]
    pallas_call x0 -> x4, Pallas kernels: none -> 62.5 us  [the longest x1 38.8 us: expert_backward(): pl.pallas_call(lambda *refs: expert_kernel(chunks, *refs), grid=(chunks +...]
    dot_general x4 -> x0, matrix products: 51.5 us -> none  [the longest x1 18.6 us: expert_backward(): lax.dot_general(gate_grad, gate_mat, (((1,), (1,)), ((), ())), preferred_...]
    reshape x6 -> x0, local copies, waits for them, and re-layouts: 39.4 us -> none  [the longest x1 8.03 us: body(): slot_rows = returned.reshape(experts_count * span, returned.shape[2])]
    all_to_all x3 -> x1, starting transfers between devices: 35.3 us -> 6.42 us  [exchange(): lax.all_to_all(parts, 'ep', split_axis=0, concat_axis=0, tiled=True)]
    gather x3 -> x0, local copies, waits for them, and re-layouts: 27 us -> none  [the longest x1 16.7 us: body(): jnp.take(slot_rows, slot_index, axis=0).astype(jnp.float32)]
    another operation x2 -> x0, other arithmetic: 18 us -> none
  transfers between devices with their start and end apart: 3 -> 2, of which waited for: 3 -> 2; matrix products, arithmetic and copies ran while one was open for 5% -> 0% of each run, Pallas kernels for 0% -> 1%
where the time goes in v1:
time: 252 us; the launch traced here: 247 us
  blocking collectives  117 us (46%)
  Pallas kernels  62.5 us (25%)
  waiting for transfers between devices  56.4 us (22%)
  starting transfers between devices  8.71 us (3%)
    all_to_all x1, blocking collectives, exchange(): lax.all_to_all(parts, 'ep', split_axis=0, concat_axis=0, tiled=True)  117 us
    all_to_all x1, waiting for transfers between devices, exchange(): lax.all_to_all(parts, 'ep', split_axis=0, concat_axis=0, tiled=True)  54.3 us
    pallas_call x1, Pallas kernels, expert_backward(): pl.pallas_call(lambda *refs: expert_kernel(chunks, *refs), grid=(chunks +...  38.8 us
    pallas_call x1, Pallas kernels, dispatch(): pl.pallas_call(lambda *refs: dispatch_kernel(experts, *refs), grid=(2 * b...  12.8 us
    pallas_call x1, Pallas kernels, combine(): pl.pallas_call(combine_kernel, grid=(blocks,), in_specs=[pl.BlockSpec(mai...  8.16 us
    all_to_all x1, starting transfers between devices, exchange(): lax.all_to_all(parts, 'ep', split_axis=0, concat_axis=0, tiled=True)  6.42 us
  transfers between devices with their start and end apart: 2, of which 2 were waited for; matrix products, arithmetic and copies ran while one was open for 0% of the time, Pallas kernels for 1%

profile of v1, /device:TPU:1, one launch (start us, length us, event | category | flops | bytes accessed | tf_op | source)
XLA Modules:
  0.0 247.5 jit_solution(15922470312266702577)
XLA Ops:
  0.0 12.8 %dispatch.1 = bf16[512,8960]{1,0:T(8,128)(2,1)} custom-call(s32[1]{0:T(128)} %bitcast.refs_0_, s32[8,128]{1,0:T(8,128)} %bitcast.18, bf16[128,3584]{1,0:T(8,128)(2,1)} %refs_2_.1, bf16[128,3584]{1,0:T(8,128)(2,1)} %refs_3_.1), custom_call_target="tpu_custom_call" | custom-call | tf_op jit(solution)/shard_map/dispatch/pallas_call | solution.py:68
  12.8 116.5 %all_to_all.10 = bf16[64,8,8960]{2,1,0:T(8,128)(2,1)} all-to-all(bf16[64,8,8960]{2,1,0:T(8,128)(2,1)} %bitcast.10), channel_id=1, replica_groups=mesh['ep'=64,'dp'=2] {'ep'}, dimensions={0} | all-to-all | bytes 18350080 | tf_op jit(solution)/shard_map/all_to_all | solution.py:246
  129.3 38.8 %expert_backward.1 = bf16[512,4480]{1,0:T(8,128)(2,1)} custom-call(bf16[512,8960]{1,0:T(8,128)(2,1)} %bitcast.11, bf16[3584,1024]{1,0:T(8,128)(2,1)} %bitcast.12, bf16[3584,1024]{1,0:T(8,128)(2,1)} %bitcast.14, bf16[1024,3584]{1,0:T(8,128)(2,1)} %bitcast.17, bf16[3584,1024]{1,0:T(8,128)(2,1)} %bitcast.13, bf16[3584,1024]{1,0:T(8,128)(2,1)} %bitcast.15), custom_call_target="tpu_custom_call" | custom-call | tf_op jit(solution)/shard_map/expert_backward/pallas_call | solution.py:188
  168.1 6.4 %all-to-all-start.1 = ((bf16[64,8,4480]{2,1,0:T(8,128)(2,1)}), bf16[64,8,4480]{2,1,0:T(8,128)(2,1)}, u32[]{:S(2)}, u32[]{:S(2)}) async-start(bf16[64,8,4480]{2,1,0:T(8,128)(2,1)} %bitcast.16), calls=%async_computation.1 | async-start | bytes 9175040 | tf_op jit(solution)/shard_map/all_to_all | solution.py:246
  174.6 2.7 %combine_weights.1 = (bf16[256,512]{1,0:T(8,128)(2,1)}, bf16[1024,512]{1,0:T(8,128)(2,1)}) custom-call(s32[1]{0:T(128)} %bitcast.refs_0_, s32[8,128]{1,0:T(8,128)} %bitcast.19, f32[8,128]{1,0:T(8,128)} %bitcast.20), custom_call_target="tpu_custom_call" | custom-call | tf_op jit(solution)/shard_map/combine_weights/pallas_call | solution.py:106
  177.3 54.3 %all-to-all-done.1 = bf16[64,8,4480]{2,1,0:T(8,128)(2,1)} async-done(((bf16[64,8,4480]{2,1,0:T(8,128)(2,1)}), bf16[64,8,4480]{2,1,0:T(8,128)(2,1)}, u32[]{:S(2)}, u32[]{:S(2)}) %all-to-all-start.1) | async-done | bytes 4587552 | tf_op jit(solution)/shard_map/all_to_all | solution.py:246
  231.6 8.2 %combine.1 = f32[128,3584]{1,0:T(8,128)} custom-call(bf16[256,512]{1,0:T(8,128)(2,1)} %get-tuple-element.7.main_ref, bf16[1024,512]{1,0:T(8,128)(2,1)} %get-tuple-element.8.tail_ref, bf16[512,4480]{1,0:T(8,128)(2,1)} %bitcast.9.back_ref), custom_call_target="tpu_custom_call" | custom-call | tf_op jit(solution)/shard_map/combine/pallas_call | solution.py:230
  239.8 1.2 constant_dynamic-slice_fusion
  241.0 2.3 collective-permute-start
  243.3 2.1 collective-permute-done
  245.4 2.0 add_convert_fusion
Async XLA Ops:
  168.1 63.5 %all-to-all-start.1 = ((bf16[64,8,4480]{2,1,0:T(8,128)(2,1)}), bf16[64,8,4480]{2,1,0:T(8,128)(2,1)}, u32[]{:S(2)}, u32[]{:S(2)}) async-start(bf16[64,8,4480]{2,1,0:T(8,128)(2,1)} %bitcast.16), calls=%async_computation.1 | async-start | bytes 9175040 | tf_op jit(solution)/shard_map/all_to_all | solution.py:246
  241.0 4.4 %collective-permute-start = (f32[128,1792]{1,0:T(8,128)S(1)}, f32[128,1792]{1,0:T(8,128)S(1)}, u32[]{:S(2)}, u32[]{:S(2)}) collective-permute-start(f32[128,1792]{1,0:T(8,128)S(1)} %constant_dynamic-slice_fusion), channel_id=1, source_target_pairs={{0,1},{1,0},{2,3},{3,2},{4,5},{5,4},{6,7},{7,6},{8,9},{9,8},{10,11... | collective-permute-start | bytes 2752520 | tf_op jit(solution)/shard_map/ppermute | solution.py:264

commit v2 on v1

v2 whole, which is shorter than its diff:
```python
import jax
import jax.numpy as jnp
from jax import lax
from jax.experimental import pallas as pl
from jax.experimental.pallas import tpu as pltpu
from jax.sharding import PartitionSpec as P

BF16, F32 = jnp.bfloat16, jnp.float32
TILE = 8
LATE = 2
FOLD = TILE // LATE
TRANSPOSED = (((1,), (1,)), ((), ()))


def iota(shape, dim):
    return lax.broadcasted_iota(jnp.int32, shape, dim)


def dot(a, b):
    return jnp.dot(a, b, preferred_element_type=F32)


def dot_t(a, b):
    return lax.dot_general(a, b, TRANSPOSED, preferred_element_type=F32)


def spread(experts):
    shape = (experts * TILE, experts)
    return jnp.where(iota(shape, 0) // TILE == iota(shape, 1), 1.0, 0.0).astype(BF16)


def slot_keys(ids_ref, core, experts):
    top, tokens = ids_ref.shape
    number = iota((experts, tokens), 0)
    named = ids_ref[0:1, :] == number
    for k in range(1, top):
        named = named | (ids_ref[k : k + 1, :] == number)
    before = jnp.where(iota((tokens, tokens), 0) < iota((tokens, tokens), 1), 1.0, 0.0).astype(BF16)
    rank = dot(jnp.where(named, 1.0, 0.0).astype(BF16), before)
    base = ((TILE + LATE) * core).astype(F32)
    key = jnp.where(named, rank - base, -100.0).astype(BF16)
    return dot(spread(experts), key)


def main_match(key):
    return key == (iota(key.shape, 0) % TILE).astype(F32)


def late_match(key, q):
    row = iota(key.shape, 0) % TILE
    return (key == (TILE + row % LATE).astype(F32)) & (row // LATE == q)


def dispatch_main_kernel(experts, core_ref, ids_ref, x_ref, g_ref, out_ref, select):
    step, half = pl.program_id(0), pl.num_programs(0) // 2

    @pl.when(step == 0)
    def _():
        key = slot_keys(ids_ref, core_ref[0], experts)
        select[...] = jnp.where(main_match(key), 1.0, 0.0).astype(BF16)

    @pl.when(step < half)
    def _():
        out_ref[...] = dot(select[...], x_ref[...]).astype(BF16)

    @pl.when(step >= half)
    def _():
        out_ref[...] = dot(select[...], g_ref[...]).astype(BF16)


def dispatch_main(core, ids, x, g, experts):
    tokens, features = x.shape
    blocks, rows = FOLD, experts * TILE
    width = features // blocks
    return pl.pallas_call(
        lambda *refs: dispatch_main_kernel(experts, *refs),
        grid=(2 * blocks,),
        in_specs=[
            pl.BlockSpec(memory_space=pltpu.SMEM),
            pl.BlockSpec(ids.shape, lambda s: (0, 0)),
            pl.BlockSpec((tokens, width), lambda s: (0, jnp.minimum(s, blocks - 1))),
            pl.BlockSpec((tokens, width), lambda s: (0, jnp.maximum(s - blocks, 0))),
        ],
        out_specs=pl.BlockSpec((rows, width), lambda s: (0, s)),
        out_shape=jax.ShapeDtypeStruct((rows, 2 * features), BF16),
        scratch_shapes=[pltpu.VMEM((rows, tokens), BF16)],
        name="dispatch_main",
    )(core, ids, x, g)


def dispatch_late_kernel(experts, core_ref, ids_ref, x_ref, g_ref, out_ref):
    key = slot_keys(ids_ref, core_ref[0], experts)
    width = out_ref.shape[1] // 2
    select = jnp.concatenate([jnp.where(late_match(key, q), 1.0, 0.0).astype(BF16) for q in range(FOLD)], 1)
    for n, ref in enumerate((x_ref, g_ref)):
        stacked = jnp.concatenate([ref[:, q * width : (q + 1) * width] for q in range(FOLD)], 0)
        out_ref[:, n * width : (n + 1) * width] = dot(select, stacked).astype(BF16)


def dispatch_late(core, ids, x, g, experts):
    features = x.shape[1]
    return pl.pallas_call(
        lambda *refs: dispatch_late_kernel(experts, *refs),
        in_specs=[pl.BlockSpec(memory_space=pltpu.SMEM)] + [pl.BlockSpec(memory_space=pltpu.VMEM)] * 3,
        out_shape=jax.ShapeDtypeStruct((experts * TILE, 2 * features // FOLD), BF16),
        name="dispatch_late",
    )(core, ids, x, g)


def weights_kernel(experts, core_ref, ids_ref, probs_ref, main_ref, late_ref):
    top, tokens = ids_ref.shape
    key = slot_keys(ids_ref, core_ref[0], experts)
    number = iota((experts, tokens), 0)
    prob = jnp.zeros((experts, tokens), F32)
    for k in range(top):
        prob = prob + jnp.where(ids_ref[k : k + 1, :] == number, probs_ref[k : k + 1, :], 0.0)
    high = prob.astype(BF16)
    low = (prob - high.astype(F32)).astype(BF16)
    for n, part in enumerate((high, low)):
        wide = dot(spread(experts), part)
        main_ref[n * tokens : (n + 1) * tokens, :] = jnp.where(main_match(key), wide, 0.0).T.astype(BF16)
        for q in range(FOLD):
            at = (2 * q + n) * tokens
            late_ref[at : at + tokens, :] = jnp.where(late_match(key, q), wide, 0.0).T.astype(BF16)


def combine_weights(core, ids, probs, experts):
    tokens = ids.shape[1]
    rows = experts * TILE
    return pl.pallas_call(
        lambda *refs: weights_kernel(experts, *refs),
        in_specs=[pl.BlockSpec(memory_space=pltpu.SMEM)] + [pl.BlockSpec(memory_space=pltpu.VMEM)] * 2,
        out_shape=[
            jax.ShapeDtypeStruct((2 * tokens, rows), BF16),
            jax.ShapeDtypeStruct((2 * FOLD * tokens, rows), BF16),
        ],
        name="combine_weights",
    )(core, ids, probs)


def gradients(gate_pre, up_pre, hidden_grad):
    sigmoid = jax.nn.sigmoid(gate_pre)
    common = hidden_grad * sigmoid
    return (common * up_pre * (1.0 + gate_pre * (1.0 - sigmoid))).astype(BF16), (common * gate_pre).astype(BF16)


def expert_main_kernel(chunks, x_ref, g_ref, gate_cols, up_cols, down_rows, gate_rows, up_rows, out_ref, gg_s, ug_s):
    step = pl.program_id(0)

    @pl.when(step < chunks)
    def _():
        gate_pre = dot(x_ref[...], gate_cols[...])
        up_pre = dot(x_ref[...], up_cols[...])
        hidden_grad = dot_t(g_ref[...], down_rows[...])
        gg_s[step], ug_s[step] = gradients(gate_pre, up_pre, hidden_grad)

    @pl.when(step >= chunks)
    def _():
        gg = jnp.concatenate([gg_s[c] for c in range(chunks)], 1)
        ug = jnp.concatenate([ug_s[c] for c in range(chunks)], 1)
        out_ref[...] = (dot_t(gg, gate_rows[...]) + dot_t(ug, up_rows[...])).astype(BF16)


def expert_main(packets, gate, up, down):
    features, hidden = gate.shape
    rows = packets.shape[0]
    blocks, width = FOLD, 256
    wide, chunks = features // blocks, hidden // width
    first = lambda s: jnp.minimum(s, chunks - 1)
    second = lambda s: jnp.maximum(s - chunks, 0)
    return pl.pallas_call(
        lambda *refs: expert_main_kernel(chunks, *refs),
        grid=(chunks + blocks,),
        in_specs=[
            pl.BlockSpec((rows, features), lambda s: (0, 0), pipeline_mode=pl.Buffered(1)),
            pl.BlockSpec((rows, features), lambda s: (0, 1), pipeline_mode=pl.Buffered(1)),
            pl.BlockSpec((features, width), lambda s: (0, first(s))),
            pl.BlockSpec((features, width), lambda s: (0, first(s))),
            pl.BlockSpec((width, features), lambda s: (first(s), 0)),
            pl.BlockSpec((wide, hidden), lambda s: (second(s), 0)),
            pl.BlockSpec((wide, hidden), lambda s: (second(s), 0)),
        ],
        out_specs=pl.BlockSpec((rows, wide), lambda s: (0, second(s))),
        out_shape=jax.ShapeDtypeStruct((rows, features + wide), BF16),
        scratch_shapes=[pltpu.VMEM((chunks, rows, width), BF16)] * 2,
        compiler_params=pltpu.CompilerParams(vmem_limit_bytes=60 * 1024 * 1024),
        name="expert_main",
    )(packets, packets, gate, up, down, gate, up)


def unfold_matrix(rows, transposed):
    unfolded, packed = iota((rows, rows), int(transposed)), iota((rows, rows), 1 - int(transposed))
    per = rows // FOLD
    q, rest = unfolded // per, unfolded % per
    at = (rest // LATE) * TILE + LATE * q + rest % LATE
    return jnp.where(at == packed, 1.0, 0.0).astype(BF16)


def expert_late_kernel(packet_ref, gate_ref, up_ref, down_ref, held_ref, out_ref, x_s, g_s, total):
    del held_ref
    step, last = pl.program_id(0), pl.num_programs(0) - 1
    rows = packet_ref.shape[0]
    per = rows // FOLD
    wide = out_ref.shape[1]

    @pl.when(step == 0)
    def _():
        unfolded = dot(unfold_matrix(rows, False), packet_ref[...]).astype(BF16)
        for n, dst in enumerate((x_s, g_s)):
            for q in range(FOLD):
                dst[:, q * wide : (q + 1) * wide] = unfolded[q * per : (q + 1) * per, n * wide : (n + 1) * wide]
        total[...] = jnp.zeros_like(total)

    gate_pre = dot(x_s[...], gate_ref[...])
    up_pre = dot(x_s[...], up_ref[...])
    hidden_grad = dot_t(g_s[...], down_ref[...])
    gate_grad, up_grad = gradients(gate_pre, up_pre, hidden_grad)
    total[...] += dot_t(gate_grad, gate_ref[...]) + dot_t(up_grad, up_ref[...])

    @pl.when(step == last)
    def _():
        stacked = jnp.concatenate([total[:, q * wide : (q + 1) * wide].astype(BF16) for q in range(FOLD)], 0)
        out_ref[...] = dot(unfold_matrix(rows, True), stacked).astype(BF16)


def expert_late(packets, gate, up, down, held):
    features, hidden = gate.shape
    rows = packets.shape[0]
    width, wide = 256, features // FOLD
    return pl.pallas_call(
        expert_late_kernel,
        grid=(hidden // width,),
        in_specs=[
            pl.BlockSpec(packets.shape, lambda s: (0, 0)),
            pl.BlockSpec((features, width), lambda s: (0, s)),
            pl.BlockSpec((features, width), lambda s: (0, s)),
            pl.BlockSpec((width, features), lambda s: (s, 0)),
            pl.BlockSpec(memory_space=pl.ANY),
        ],
        out_specs=pl.BlockSpec((rows, wide), lambda s: (0, FOLD)),
        out_shape=jax.ShapeDtypeStruct(held.shape, BF16),
        scratch_shapes=[pltpu.VMEM((rows // FOLD, features), BF16)] * 2 + [pltpu.VMEM((rows // FOLD, features), F32)],
        input_output_aliases={4: 0},
        compiler_params=pltpu.CompilerParams(vmem_limit_bytes=60 * 1024 * 1024),
        name="expert_late",
    )(packets, gate, up, down, held)


def combine_kernel(half_ref, main_ref, late_ref, back_ref, late_back_ref, out_ref):
    del half_ref
    tokens = out_ref.shape[0]
    both = dot(main_ref[...], back_ref[...]) + dot(late_ref[...], late_back_ref[...])
    out_ref[...] = both[:tokens] + both[tokens:]


def combine(half, main, late, back):
    rows, width = back.shape
    wide = width // (FOLD + 1)
    tokens, steps = main.shape[0] // 2, FOLD // 2
    return pl.pallas_call(
        combine_kernel,
        grid_spec=pltpu.PrefetchScalarGridSpec(
            num_scalar_prefetch=1,
            grid=(steps,),
            in_specs=[
                pl.BlockSpec(main.shape, lambda s, half: (0, 0)),
                pl.BlockSpec((2 * tokens, rows), lambda s, half: (steps * half[0] + s, 0)),
                pl.BlockSpec((rows, wide), lambda s, half: (0, steps * half[0] + s)),
                pl.BlockSpec((rows, wide), lambda s, half: (0, FOLD)),
            ],
            out_specs=pl.BlockSpec((tokens, wide), lambda s, half: (0, s)),
        ),
        out_shape=jax.ShapeDtypeStruct((tokens, steps * wide), F32),
        name="combine",
    )(half, main, late, back, back)


def exchange(packets, experts):
    parts = packets.reshape(experts, TILE, -1)
    return lax.all_to_all(parts, "ep", split_axis=0, concat_axis=0, tiled=True).reshape(packets.shape)


def body(layer_input, out_grad, expert_ids, gate_probs, gate_proj, up_proj, down_proj):
    experts = lax.axis_size("ep")
    core = jnp.full((1,), lax.axis_index("dp"), jnp.int32)
    ids = expert_ids.T
    gate, up, down = gate_proj[0], up_proj[0], down_proj[0]
    arrived = exchange(dispatch_main(core, ids, layer_input, out_grad, experts), experts)
    late_arrived = exchange(dispatch_late(core, ids, layer_input, out_grad, experts), experts)
    main, late = combine_weights(core, ids, gate_probs.T, experts)
    back = expert_late(late_arrived, gate, up, down, expert_main(arrived, gate, up, down))
    returned = exchange(back, experts)
    crossing = lax.ppermute(combine(1 - core, main, late, returned), "dp", ((0, 1), (1, 0)))
    return (combine(core, main, late, returned) + crossing).astype(BF16)


def solution(mesh):
    rows = P("ep", None)
    mats = P("ep", None, None)
    return jax.shard_map(body, mesh=mesh, in_specs=(rows,) * 4 + (mats,) * 3, out_specs=P("ep", "dp"), check_vma=False)
```

time: 252 us -> 253 us (level); the launches traced: 247 us -> 252 us
  blocking collectives: 117 us -> 0 us
  waiting for transfers between devices: 56.4 us -> 139 us
  starting transfers between devices: 8.71 us -> 38 us
  Pallas kernels: 62.5 us -> 72.3 us
    all_to_all x1 -> x0, blocking collectives: 117 us -> none  [exchange(): lax.all_to_all(parts, 'ep', split_axis=0, concat_axis=0, tiled=True)]
    all_to_all x1 -> x3, waiting for transfers between devices: 54.3 us -> 139 us  [exchange(): lax.all_to_all(parts, 'ep', split_axis=0, concat_axis=0, tiled=True)]
    all_to_all x1 -> x3, starting transfers between devices: 6.42 us -> 34 us  [exchange(): lax.all_to_all(parts, 'ep', split_axis=0, concat_axis=0, tiled=True)]
    pallas_call x3 -> x6, Pallas kernels: 59.8 us -> 69.6 us  [the longest x1 29.5 us: expert_main(): pl.pallas_call(lambda *refs: expert_main_kernel(chunks, *refs), grid=(chu...]
  transfers between devices with their start and end apart: 2 -> 4, of which waited for: 2 -> 2; matrix products, arithmetic and copies ran while one was open for 0% -> 0% of each run, Pallas kernels for 1% -> 16%
where the time goes in v2:
time: 253 us; the launch traced here: 252 us
  waiting for transfers between devices  139 us (55%)
  Pallas kernels  72.3 us (29%)
  starting transfers between devices  38 us (15%)
    all_to_all x3, waiting for transfers between devices, exchange(): lax.all_to_all(parts, 'ep', split_axis=0, concat_axis=0, tiled=True)  139 us
    all_to_all x3, starting transfers between devices, exchange(): lax.all_to_all(parts, 'ep', split_axis=0, concat_axis=0, tiled=True)  34 us
    pallas_call x1, Pallas kernels, expert_main(): pl.pallas_call(lambda *refs: expert_main_kernel(chunks, *refs), grid=(chu...  29.5 us
    pallas_call x1, Pallas kernels, expert_late(): pl.pallas_call(expert_late_kernel, grid=(hidden // width,), in_specs=[pl....  19.7 us
    pallas_call x1, Pallas kernels, dispatch_main(): pl.pallas_call(lambda *refs: dispatch_main_kernel(experts, *refs), grid=(...  8.4 us
    pallas_call x2, Pallas kernels, combine(): pl.pallas_call(combine_kernel, grid_spec=pltpu.PrefetchScalarGridSpec(num...  7.7 us
  transfers between devices with their start and end apart: 4, of which 2 were waited for; matrix products, arithmetic and copies ran while one was open for 0% of the time, Pallas kernels for 16%

profile of v2, /device:TPU:1, one launch (start us, length us, event | category | flops | bytes accessed | tf_op | source)
XLA Modules:
  0.0 252.2 jit_solution(17297543246673060780)
XLA Ops:
  0.0 8.4 %dispatch_main.1 = bf16[512,7168]{1,0:T(8,128)(2,1)} custom-call(s32[1]{0:T(128)} %bitcast.refs_0_.half_ref, s32[8,128]{1,0:T(8,128)} %bitcast.24, bf16[128,3584]{1,0:T(8,128)(2,1)} %refs_2_.3, bf16[128,3584]{1,0:T(8,128)(2,1)} %refs_3_.3), custom_call_target="tpu_custom_call" | custom-call | tf_op jit(solution)/shard_map/dispatch_main/pallas_call | solution.py:75
  8.4 12.2 %all-to-all-start.1 = ((bf16[64,8,7168]{2,1,0:T(8,128)(2,1)}), bf16[64,8,7168]{2,1,0:T(8,128)(2,1)}, u32[]{:S(2)}, u32[]{:S(2)}) async-start(bf16[64,8,7168]{2,1,0:T(8,128)(2,1)} %bitcast.19), calls=%async_computation.1 | async-start | bytes 14680064 | tf_op jit(solution)/shard_map/all_to_all | solution.py:280
  20.6 4.3 %dispatch_late.1 = bf16[512,1792]{1,0:T(8,128)(2,1)} custom-call(s32[1]{0:T(128)} %bitcast.refs_0_.half_ref, s32[8,128]{1,0:T(8,128)} %bitcast.25, bf16[128,3584]{1,0:T(8,128)(2,1)} %refs_2_.3, bf16[128,3584]{1,0:T(8,128)(2,1)} %refs_3_.3), custom_call_target="tpu_custom_call" | custom-call | tf_op jit(solution)/shard_map/dispatch_late/pallas_call | solution.py:102
  24.8 88.2 %all-to-all-done.1 = bf16[64,8,7168]{2,1,0:T(8,128)(2,1)} async-done(((bf16[64,8,7168]{2,1,0:T(8,128)(2,1)}), bf16[64,8,7168]{2,1,0:T(8,128)(2,1)}, u32[]{:S(2)}, u32[]{:S(2)}) %all-to-all-start.1) | async-done | bytes 7340064 | tf_op jit(solution)/shard_map/all_to_all | solution.py:280
  113.1 11.7 %all-to-all-start = ((bf16[64,8,1792]{2,1,0:T(8,128)(2,1)}), bf16[64,8,1792]{2,1,0:T(8,128)(2,1)S(1)}, u32[]{:S(2)}, u32[]{:S(2)}) async-start(bf16[64,8,1792]{2,1,0:T(8,128)(2,1)} %bitcast.22), calls=%async_computation | async-start | bytes 3670016 | tf_op jit(solution)/shard_map/all_to_all | solution.py:280
  124.8 29.5 %expert_main.1.held_ref = bf16[512,4480]{1,0:T(8,128)(2,1)} custom-call(bf16[512,7168]{1,0:T(8,128)(2,1)} %bitcast.9.refs_0_.refs_1_, bf16[512,7168]{1,0:T(8,128)(2,1)} %bitcast.9.refs_0_.refs_1_, bf16[3584,1024]{1,0:T(8,128)(2,1)} %bitcast.12, bf16[3584,1024]{1,0:T(8,128)(2,1)} %bitcast.15, bf16[1024,3584]{1,0:T(8,128)(2,1)} %bitcast.20, ...), custom_call_target="tpu_custom_call" | custom-call | tf_op jit(solution)/shard_map/expert_main/pallas_call | solution.py:171
  154.3 0.0 all-to-all-done
  154.3 0.0 copy-start
  154.3 1.2 copy-done
  155.5 19.7 %expert_late.1 = bf16[512,4480]{1,0:T(8,128)(2,1)} custom-call(bf16[512,1792]{1,0:T(8,128)(2,1)} %bitcast.23, bf16[3584,1024]{1,0:T(8,128)(2,1)} %bitcast.14, bf16[3584,1024]{1,0:T(8,128)(2,1)} %bitcast.17, bf16[1024,3584]{1,0:T(8,128)(2,1)} %bitcast.21, bf16[512,4480]{1,0:T(8,128)(2,1)} %expert_main.1.held_ref), custom_call_target="tpu_custom_call", output_to_operand_aliasing={{}: (4, {})} | custom-call | tf_op jit(solution)/shard_map/expert_late/pallas_call | solution.py:230
  175.2 10.2 %all-to-all-start.2 = ((bf16[64,8,4480]{2,1,0:T(8,128)(2,1)}), bf16[64,8,4480]{2,1,0:T(8,128)(2,1)}, u32[]{:S(2)}, u32[]{:S(2)}) async-start(bf16[64,8,4480]{2,1,0:T(8,128)(2,1)} %bitcast.18), calls=%async_computation.2 | async-start | bytes 9175040 | tf_op jit(solution)/shard_map/all_to_all | solution.py:280
  185.4 2.7 %combine_weights.1 = (bf16[256,512]{1,0:T(8,128)(2,1)}, bf16[1024,512]{1,0:T(8,128)(2,1)}) custom-call(s32[1]{0:T(128)} %bitcast.refs_0_.half_ref, s32[8,128]{1,0:T(8,128)} %bitcast.26, f32[8,128]{1,0:T(8,128)} %bitcast.27), custom_call_target="tpu_custom_call" | custom-call | tf_op jit(solution)/shard_map/combine_weights/pallas_call | solution.py:130
  188.1 50.4 %all-to-all-done.2 = bf16[64,8,4480]{2,1,0:T(8,128)(2,1)} async-done(((bf16[64,8,4480]{2,1,0:T(8,128)(2,1)}), bf16[64,8,4480]{2,1,0:T(8,128)(2,1)}, u32[]{:S(2)}, u32[]{:S(2)}) %all-to-all-start.2) | async-done | bytes 4587552 | tf_op jit(solution)/shard_map/all_to_all | solution.py:280
  238.5 3.8 %combine.3 = f32[128,1792]{1,0:T(8,128)} custom-call(s32[1]{0:T(128)S(6)} %sub.3.half_ref, bf16[256,512]{1,0:T(8,128)(2,1)} %get-tuple-element.7.main_ref, bf16[1024,512]{1,0:T(8,128)(2,1)} %get-tuple-element.8.late_ref, bf16[512,4480]{1,0:T(8,128)(2,1)} %bitcast.11.back_ref.late_back_ref, bf16[512,4480]{1,0:T(8,128)(2,1)} %bitcast.11.back_ref.late_back_ref), custom_call_target="tpu_custom_call" | custom-call | tf_op jit(solution)/shard_map/combine/pallas_call | solution.py:260
  242.3 4.0 %collective-permute-start = (f32[128,1792]{1,0:T(8,128)}, f32[128,1792]{1,0:T(8,128)S(1)}, u32[]{:S(2)}, u32[]{:S(2)}) collective-permute-start(f32[128,1792]{1,0:T(8,128)} %combine.3), channel_id=1, source_target_pairs={{0,1},{1,0},{2,3},{3,2},{4,5},{5,4},{6,7},{7,6},{8,9},{9,8},{10,11... | collective-permute-start | bytes 2752520 | tf_op jit(solution)/shard_map/ppermute | solution.py:293
  246.3 3.9 %combine.2 = f32[128,1792]{1,0:T(8,128)} custom-call(s32[1]{0:T(128)} %bitcast.refs_0_.half_ref, bf16[256,512]{1,0:T(8,128)(2,1)} %get-tuple-element.7.main_ref, bf16[1024,512]{1,0:T(8,128)(2,1)} %get-tuple-element.8.late_ref, bf16[512,4480]{1,0:T(8,128)(2,1)} %bitcast.11.back_ref.late_back_ref, bf16[512,4480]{1,0:T(8,128)(2,1)} %bitcast.11.back_ref.late_back_ref), custom_call_target="tpu_custom_call" | custom-call | tf_op jit(solution)/shard_map/combine/pallas_call | solution.py:260
  250.2 0.0 collective-permute-done
  250.2 2.0 add_convert_fusion
Async XLA Ops:
  8.4 104.7 %all-to-all-start.1 = ((bf16[64,8,7168]{2,1,0:T(8,128)(2,1)}), bf16[64,8,7168]{2,1,0:T(8,128)(2,1)}, u32[]{:S(2)}, u32[]{:S(2)}) async-start(bf16[64,8,7168]{2,1,0:T(8,128)(2,1)} %bitcast.19), calls=%async_computation.1 | async-start | bytes 14680064 | tf_op jit(solution)/shard_map/all_to_all | solution.py:280
  113.1 41.2 %all-to-all-start = ((bf16[64,8,1792]{2,1,0:T(8,128)(2,1)}), bf16[64,8,1792]{2,1,0:T(8,128)(2,1)S(1)}, u32[]{:S(2)}, u32[]{:S(2)}) async-start(bf16[64,8,1792]{2,1,0:T(8,128)(2,1)} %bitcast.22), calls=%async_computation | async-start | bytes 3670016 | tf_op jit(solution)/shard_map/all_to_all | solution.py:280
  154.3 1.2 copy-start
  175.2 63.3 %all-to-all-start.2 = ((bf16[64,8,4480]{2,1,0:T(8,128)(2,1)}), bf16[64,8,4480]{2,1,0:T(8,128)(2,1)}, u32[]{:S(2)}, u32[]{:S(2)}) async-start(bf16[64,8,4480]{2,1,0:T(8,128)(2,1)} %bitcast.18), calls=%async_computation.2 | async-start | bytes 9175040 | tf_op jit(solution)/shard_map/all_to_all | solution.py:280
  242.3 7.8 %collective-permute-start = (f32[128,1792]{1,0:T(8,128)}, f32[128,1792]{1,0:T(8,128)S(1)}, u32[]{:S(2)}, u32[]{:S(2)}) collective-permute-start(f32[128,1792]{1,0:T(8,128)} %combine.3), channel_id=1, source_target_pairs={{0,1},{1,0},{2,3},{3,2},{4,5},{5,4},{6,7},{7,6},{8,9},{9,8},{10,11... | collective-permute-start | bytes 2752520 | tf_op jit(solution)/shard_map/ppermute | solution.py:293

commit v3 on v2

v3 whole, which is shorter than its diff:
```python
import jax
import jax.numpy as jnp
from jax import lax
from jax.experimental import pallas as pl
from jax.experimental.pallas import tpu as pltpu
from jax.sharding import PartitionSpec as P

BF16, F32 = jnp.bfloat16, jnp.float32
TILE = 8
LATE = 2
FOLD = TILE // LATE
WAIT, HOLD = 51500, 17000
VMEM_MIB = 58
TRANSPOSED = (((1,), (1,)), ((), ()))


def iota(shape, dim):
    return lax.broadcasted_iota(jnp.int32, shape, dim)


def dot(a, b):
    return jnp.dot(a, b, preferred_element_type=F32)


def dot_t(a, b):
    return lax.dot_general(a, b, TRANSPOSED, preferred_element_type=F32)


def spread(experts):
    shape = (experts * TILE, experts)
    return jnp.where(iota(shape, 0) // TILE == iota(shape, 1), 1.0, 0.0).astype(BF16)


def slot_keys(ids_ref, core, experts):
    top, tokens = ids_ref.shape
    number = iota((experts, tokens), 0)
    named = ids_ref[0:1, :] == number
    for k in range(1, top):
        named = named | (ids_ref[k : k + 1, :] == number)
    before = jnp.where(iota((tokens, tokens), 0) < iota((tokens, tokens), 1), 1.0, 0.0).astype(BF16)
    rank = dot(jnp.where(named, 1.0, 0.0).astype(BF16), before)
    base = ((TILE + LATE) * core).astype(F32)
    key = jnp.where(named, rank - base, -100.0).astype(BF16)
    return dot(spread(experts), key)


def main_match(key):
    return key == (iota(key.shape, 0) % TILE).astype(F32)


def late_match(key, q):
    row = iota(key.shape, 0) % TILE
    return (key == (TILE + row % LATE).astype(F32)) & (row // LATE == q)


def dispatch_kernel(experts, core_ref, ids_ref, x_ref, g_ref, out_ref, ready, sems):
    key = slot_keys(ids_ref, core_ref[0], experts)
    slots, _, width = ready.shape
    main = jnp.where(main_match(key), 1.0, 0.0).astype(BF16)
    late = jnp.concatenate([jnp.where(late_match(key, q), 1.0, 0.0).astype(BF16) for q in range(FOLD)], 1)
    copies = []
    for ref in (x_ref, g_ref):
        parts = [ref[:, q * width : (q + 1) * width] for q in range(FOLD)]
        for select, rows in [(main, part) for part in parts] + [(late, jnp.concatenate(parts, 0))]:
            n = len(copies)
            if n >= slots:
                copies[n - slots].wait()
            ready[n % slots] = dot(select, rows).astype(BF16)
            copies.append(pltpu.make_async_copy(ready.at[n % slots], out_ref.at[:, n * width : (n + 1) * width], sems.at[n % slots]))
            copies[n].start()
    for copy in copies[-slots:]:
        copy.wait()


def dispatch(core, ids, x, g, experts):
    rows, width = experts * TILE, x.shape[1] // FOLD
    slots = 4
    return pl.pallas_call(
        lambda *refs: dispatch_kernel(experts, *refs),
        in_specs=[pl.BlockSpec(memory_space=pltpu.SMEM)] + [pl.BlockSpec(memory_space=pltpu.VMEM)] * 3,
        out_specs=pl.BlockSpec(memory_space=pl.ANY),
        out_shape=jax.ShapeDtypeStruct((rows, 2 * (FOLD + 1) * width), BF16),
        scratch_shapes=[pltpu.VMEM((slots, rows, width), BF16), pltpu.SemaphoreType.DMA((slots,))],
        name="dispatch",
    )(core, ids, x, g)


def combine_weights(experts, core, ids_ref, probs_ref, main_ref, late_ref):
    top, tokens = ids_ref.shape
    key = slot_keys(ids_ref, core, experts)
    number = iota((experts, tokens), 0)
    prob = jnp.zeros((experts, tokens), F32)
    for k in range(top):
        prob = prob + jnp.where(ids_ref[k : k + 1, :] == number, probs_ref[k : k + 1, :], 0.0)
    high = prob.astype(BF16)
    low = (prob - high.astype(F32)).astype(BF16)
    for n, part in enumerate((high, low)):
        wide = dot(spread(experts), part)
        main_ref[n * tokens : (n + 1) * tokens, :] = jnp.where(main_match(key), wide, 0.0).T.astype(BF16)
        for q in range(FOLD):
            at = (2 * q + n) * tokens
            late_ref[at : at + tokens, :] = jnp.where(late_match(key, q), wide, 0.0).T.astype(BF16)


def pause_kernel(experts, turn, nanos, core_ref, ids_ref, probs_ref, *refs):
    main_ref, late_ref, main_s, late_s, sems = refs[-5:]
    core = core_ref[0]

    @pl.when(core == turn)
    def _():
        combine_weights(experts, core, ids_ref, probs_ref, main_s, late_s)
        copies = [
            pltpu.make_async_copy(main_s, main_ref, sems.at[0]),
            pltpu.make_async_copy(late_s, late_ref, sems.at[1]),
        ]
        for copy in copies:
            copy.start()
        for copy in copies:
            copy.wait()
        pl.delay(nanos)


def pause(turn, nanos, core, ids, probs, experts, packets, weights=()):
    tokens, rows = ids.shape[1], experts * TILE
    shapes = [jax.ShapeDtypeStruct((2 * n * tokens, rows), BF16) for n in (1, FOLD)]
    anywhere = pl.BlockSpec(memory_space=pl.ANY)
    return pl.pallas_call(
        lambda *refs: pause_kernel(experts, turn, nanos, *refs),
        in_specs=[pl.BlockSpec(memory_space=pltpu.SMEM)] + [pl.BlockSpec(memory_space=pltpu.VMEM)] * 2 + [anywhere] * (1 + len(weights)),
        out_specs=[anywhere] * 3,
        out_shape=[jax.ShapeDtypeStruct(packets.shape, packets.dtype)] + shapes,
        scratch_shapes=[pltpu.VMEM(shape.shape, BF16) for shape in shapes] + [pltpu.SemaphoreType.DMA((2,))],
        input_output_aliases={3 + n: n for n in range(1 + len(weights))},
        name="pause",
    )(core, ids, probs, packets, *weights)


def gradients(gate_pre, up_pre, hidden_grad):
    sigmoid = jax.nn.sigmoid(gate_pre)
    common = hidden_grad * sigmoid
    return (common * up_pre * (1.0 + gate_pre * (1.0 - sigmoid))).astype(BF16), (common * gate_pre).astype(BF16)


def unfold_matrix(rows, transposed):
    unfolded, packed = iota((rows, rows), int(transposed)), iota((rows, rows), 1 - int(transposed))
    per = rows // FOLD
    q, rest = unfolded // per, unfolded % per
    at = (rest // LATE) * TILE + LATE * q + rest % LATE
    return jnp.where(at == packed, 1.0, 0.0).astype(BF16)


def expert_kernel(chunks, packet_ref, gate_ref, up_ref, down_ref, out_ref, x_s, g_s, tail_s, fold_s, gate_c, up_c, down_c, gate_r, up_r, gg_s, ug_s, late_s, in_sems, col_sems, row_sems):
    step = pl.program_id(0)
    rows = packet_ref.shape[0]
    wide = out_ref.shape[1]
    width = gate_c.shape[2]
    features = FOLD * wide
    per = rows // FOLD

    def packet_copies(n, dst):
        at = n * (features + wide)
        return (
            pltpu.make_async_copy(packet_ref.at[:, at : at + features], dst.at[0:rows, :], in_sems.at[2 * n]),
            pltpu.make_async_copy(packet_ref.at[:, at + features : at + features + wide], tail_s.at[n], in_sems.at[2 * n + 1]),
        )

    def col_copies(c):
        slot, at = c % 2, pl.multiple_of(c * width, width)
        return (
            pltpu.make_async_copy(gate_ref.at[:, pl.ds(at, width)], gate_c.at[slot], col_sems.at[0, slot]),
            pltpu.make_async_copy(up_ref.at[:, pl.ds(at, width)], up_c.at[slot], col_sems.at[1, slot]),
            pltpu.make_async_copy(down_ref.at[pl.ds(at, width), :], down_c.at[slot], col_sems.at[2, slot]),
        )

    def row_copies(q):
        slot, at = q % 2, pl.multiple_of(q * wide, wide)
        return (
            pltpu.make_async_copy(gate_ref.at[pl.ds(at, wide), :], gate_r.at[slot], row_sems.at[0, slot]),
            pltpu.make_async_copy(up_ref.at[pl.ds(at, wide), :], up_r.at[slot], row_sems.at[1, slot]),
        )

    def start(copies):
        for copy in copies:
            copy.start()

    def wait(copies):
        for copy in copies:
            copy.wait()

    @pl.when(step == 0)
    def _():
        x_main, x_tail = packet_copies(0, x_s)
        g_main, g_tail = packet_copies(1, g_s)
        gate_0, up_0, down_0 = col_copies(0)
        start((x_tail, g_tail, x_main, gate_0, up_0, g_main, down_0))
        start(col_copies(1))
        unfold = unfold_matrix(rows, False)
        fold_s[...] = unfold_matrix(rows, True)
        for n, (dst, copy) in enumerate(((x_s, x_tail), (g_s, g_tail))):
            copy.wait()
            tail = dot(unfold, tail_s[n]).astype(BF16)
            for q in range(FOLD):
                dst[rows : rows + per, q * wide : (q + 1) * wide] = tail[q * per : (q + 1) * per]
        wait((x_main, gate_0, up_0))
        gate_pre = dot(x_s[...], gate_c[0])
        up_pre = dot(x_s[...], up_c[0])
        wait((g_main, down_0))
        hidden_grad = dot_t(g_s[...], down_c[0])
        gg_s[0], ug_s[0] = gradients(gate_pre, up_pre, hidden_grad)

    @pl.when((step > 0) & (step < chunks))
    def _():
        @pl.when(step < chunks - 1)
        def _():
            start(col_copies(step + 1))

        @pl.when(step == chunks - 1)
        def _():
            start(row_copies(0))
            start(row_copies(1))

        wait(col_copies(step))
        slot = step % 2
        gate_pre = dot(x_s[...], gate_c[slot])
        up_pre = dot(x_s[...], up_c[slot])
        hidden_grad = dot_t(g_s[...], down_c[slot])
        gg_s[step], ug_s[step] = gradients(gate_pre, up_pre, hidden_grad)

    @pl.when((step >= chunks) & (step < chunks + FOLD))
    def _():
        q = step - chunks
        slot = q % 2
        wait(row_copies(q))
        gg = jnp.concatenate([gg_s[c] for c in range(chunks)], 1)
        ug = jnp.concatenate([ug_s[c] for c in range(chunks)], 1)
        back = (dot_t(gg, gate_r[slot]) + dot_t(ug, up_r[slot])).astype(BF16)
        out_ref[...] = back[0:rows]
        late_s[q] = back[rows:]

        @pl.when(q < FOLD - 2)
        def _():
            start(row_copies(q + 2))

    @pl.when(step == chunks + FOLD)
    def _():
        stacked = jnp.concatenate([late_s[q] for q in range(FOLD)], 0)
        out_ref[...] = dot(fold_s[...], stacked).astype(BF16)


def expert_backward(packets, gate, up, down):
    features, hidden = gate.shape
    rows = packets.shape[0]
    items = rows + rows // FOLD
    width, wide = 256, features // FOLD
    chunks = hidden // width
    return pl.pallas_call(
        lambda *refs: expert_kernel(chunks, *refs),
        grid=(chunks + FOLD + 1,),
        in_specs=[pl.BlockSpec(memory_space=pl.ANY)] * 4,
        out_specs=pl.BlockSpec((rows, wide), lambda s: (0, jnp.maximum(s - chunks, 0))),
        out_shape=jax.ShapeDtypeStruct((rows, features + wide), BF16),
        scratch_shapes=[
            pltpu.VMEM((items, features), BF16),
            pltpu.VMEM((items, features), BF16),
            pltpu.VMEM((2, rows, wide), BF16),
            pltpu.VMEM((rows, rows), BF16),
            pltpu.VMEM((2, features, width), BF16),
            pltpu.VMEM((2, features, width), BF16),
            pltpu.VMEM((2, width, features), BF16),
            pltpu.VMEM((2, wide, hidden), BF16),
            pltpu.VMEM((2, wide, hidden), BF16),
            pltpu.VMEM((chunks, items, width), BF16),
            pltpu.VMEM((chunks, items, width), BF16),
            pltpu.VMEM((FOLD, rows // FOLD, wide), BF16),
            pltpu.SemaphoreType.DMA((4,)),
            pltpu.SemaphoreType.DMA((3, 2)),
            pltpu.SemaphoreType.DMA((2, 2)),
        ],
        compiler_params=pltpu.CompilerParams(vmem_limit_bytes=VMEM_MIB * 1024 * 1024),
        name="expert_backward",
    )(packets, gate, up, down)


def combine_kernel(core_ref, main_ref, late_ref, back_ref, late_back_ref, out_ref):
    del core_ref
    tokens = out_ref.shape[0]
    both = dot(main_ref[...], back_ref[...]) + dot(late_ref[...], late_back_ref[...])
    out_ref[...] = both[:tokens] + both[tokens:]


def combine(core, other, main, late, back):
    rows, width = back.shape
    wide = width // (FOLD + 1)
    tokens, steps = main.shape[0] // 2, FOLD // 2
    first = lambda core: steps * ((1 - core[0]) if other else core[0])
    return pl.pallas_call(
        combine_kernel,
        grid_spec=pltpu.PrefetchScalarGridSpec(
            num_scalar_prefetch=1,
            grid=(steps,),
            in_specs=[
                pl.BlockSpec(main.shape, lambda s, core: (0, 0)),
                pl.BlockSpec((2 * tokens, rows), lambda s, core: (first(core) + s, 0)),
                pl.BlockSpec((rows, wide), lambda s, core: (0, first(core) + s)),
                pl.BlockSpec((rows, wide), lambda s, core: (0, FOLD)),
            ],
            out_specs=pl.BlockSpec((tokens, wide), lambda s, core: (0, s)),
        ),
        out_shape=jax.ShapeDtypeStruct((tokens, steps * wide), F32),
        name="combine",
    )(core, main, late, back, back)


def exchange(packets, experts):
    parts = packets.reshape(experts, TILE, -1)
    return lax.all_to_all(parts, "ep", split_axis=0, concat_axis=0, tiled=True).reshape(packets.shape)


def body(layer_input, out_grad, expert_ids, gate_probs, gate_proj, up_proj, down_proj):
    experts = lax.axis_size("ep")
    core = jnp.full((1,), lax.axis_index("dp"), jnp.int32)
    ids = expert_ids.T
    packets = dispatch(core, ids, layer_input, out_grad, experts)
    probs = gate_probs.T
    packets, *weights = pause(1, WAIT, core, ids, probs, experts, packets)
    arrived, main, late = pause(0, HOLD, core, ids, probs, experts, exchange(packets, experts), weights)
    returned = exchange(expert_backward(arrived, gate_proj[0], up_proj[0], down_proj[0]), experts)
    crossing = lax.ppermute(combine(core, True, main, late, returned), "dp", ((0, 1), (1, 0)))
    return (combine(core, False, main, late, returned) + crossing).astype(BF16)


def solution(mesh):
    rows = P("ep", None)
    mats = P("ep", None, None)
    return jax.shard_map(body, mesh=mesh, in_specs=(rows,) * 4 + (mats,) * 3, out_specs=P("ep", "dp"), check_vma=False)
```

time: 253 us -> 216 us (0.85)
  waiting for transfers between devices: 139 us -> 0.01 us
  blocking collectives: 0 us -> 107 us
  starting transfers between devices: 38 us -> 0.01 us
  Pallas kernels: 72.3 us -> 106 us
    all_to_all x3 -> x0, waiting for transfers between devices: 139 us -> none  [exchange(): lax.all_to_all(parts, 'ep', split_axis=0, concat_axis=0, tiled=True)]
    all_to_all x0 -> x2, blocking collectives: none -> 107 us  [exchange(): lax.all_to_all(parts, 'ep', split_axis=0, concat_axis=0, tiled=True)]
    all_to_all x3 -> x0, starting transfers between devices: 34 us -> none  [exchange(): lax.all_to_all(parts, 'ep', split_axis=0, concat_axis=0, tiled=True)]
    pallas_call x5 -> x4, Pallas kernels: 64.6 us -> 98.5 us  [the longest x2 54.9 us: pause(): pl.pallas_call(lambda *refs: pause_kernel(experts, turn, nanos, *refs), i...]
    ppermute x1, starting transfers between devices: 3.97 us -> 0.01 us  [body(): lax.ppermute(combine(core, True, main, late, returned), 'dp', ((0, 1), (1...]
  transfers between devices with their start and end apart: 4 -> 1, of which waited for: 2 -> 0; matrix products, arithmetic and copies ran while one was open for 0% -> 0% of each run, Pallas kernels for 16% -> 2%
where the time goes in v3:
time: 216 us
  blocking collectives  107 us (50%)
  Pallas kernels  106 us (49%)
    all_to_all x2, blocking collectives, exchange(): lax.all_to_all(parts, 'ep', split_axis=0, concat_axis=0, tiled=True)  107 us
    pallas_call x2, Pallas kernels, pause(): pl.pallas_call(lambda *refs: pause_kernel(experts, turn, nanos, *refs), i...  54.9 us
    pallas_call x1, Pallas kernels, expert_backward(): pl.pallas_call(lambda *refs: expert_kernel(chunks, *refs), grid=(chunks +...  36.2 us
    pallas_call x2, Pallas kernels, combine(): pl.pallas_call(combine_kernel, grid_spec=pltpu.PrefetchScalarGridSpec(num...  7.78 us
    pallas_call x1, Pallas kernels, dispatch(): pl.pallas_call(lambda *refs: dispatch_kernel(experts, *refs), in_specs=[p...  7.36 us
  transfers between devices with their start and end apart: 1, of which 0 were waited for; matrix products, arithmetic and copies ran while one was open for 0% of the time, Pallas kernels for 2%

profile of v3, /device:TPU:1, one launch (start us, length us, event | category | flops | bytes accessed | tf_op | source)
XLA Modules:
  0.0 215.5 jit_solution(491129372237810404)
XLA Ops:
  0.0 7.4 %dispatch.1.refs_3_ = bf16[512,8960]{1,0:T(8,128)(2,1)} custom-call(s32[1]{0:T(128)} %bitcast.refs_0_.core_ref, s32[8,128]{1,0:T(8,128)} %bitcast.20, bf16[128,3584]{1,0:T(8,128)(2,1)} %refs_2_.1, bf16[128,3584]{1,0:T(8,128)(2,1)} %refs_3_.1), custom_call_target="tpu_custom_call" | custom-call | tf_op jit(solution)/shard_map/dispatch/pallas_call | solution.py:78
  7.4 54.2 %pause.2 = (bf16[512,8960]{1,0:T(8,128)(2,1)}, bf16[256,512]{1,0:T(8,128)(2,1)}, bf16[1024,512]{1,0:T(8,128)(2,1)}) custom-call(s32[1]{0:T(128)} %bitcast.refs_0_.core_ref, s32[8,128]{1,0:T(8,128)} %bitcast.21, f32[8,128]{1,0:T(8,128)} %bitcast.23, bf16[512,8960]{1,0:T(8,128)(2,1)} %dispatch.1.refs_3_), custom_call_target="tpu_custom_call", output_to_operand_aliasing={{0}: (3, {})} | custom-call | tf_op jit(solution)/shard_map/pause/pallas_call | solution.py:127
  61.6 69.1 %all_to_all.10 = bf16[64,8,8960]{2,1,0:T(8,128)(2,1)} all-to-all(bf16[64,8,8960]{2,1,0:T(8,128)(2,1)} %bitcast.15), channel_id=1, replica_groups=mesh['ep'=64,'dp'=2] {'ep'}, dimensions={0} | all-to-all | bytes 18350080 | tf_op jit(solution)/shard_map/all_to_all | solution.py:316
  130.6 0.7 pause.3
  131.4 36.2 %expert_backward.1 = bf16[512,4480]{1,0:T(8,128)(2,1)} custom-call(bf16[512,8960]{1,0:T(8,128)(2,1)} %get-tuple-element.16.refs_0_, bf16[3584,1024]{1,0:T(8,128)(2,1)} %bitcast.17, bf16[3584,1024]{1,0:T(8,128)(2,1)} %bitcast.18, bf16[1024,3584]{1,0:T(8,128)(2,1)} %bitcast.19), custom_call_target="tpu_custom_call" | custom-call | tf_op jit(solution)/shard_map/expert_backward/pallas_call | solution.py:256
  167.6 38.2 %all_to_all.11 = bf16[64,8,4480]{2,1,0:T(8,128)(2,1)} all-to-all(bf16[64,8,4480]{2,1,0:T(8,128)(2,1)} %bitcast.16), channel_id=1, replica_groups=mesh['ep'=64,'dp'=2] {'ep'}, dimensions={0} | all-to-all | bytes 9175040 | tf_op jit(solution)/shard_map/all_to_all | solution.py:316
  205.7 3.9 %combine.3 = f32[128,1792]{1,0:T(8,128)} custom-call(s32[1]{0:T(128)} %bitcast.refs_0_.core_ref, bf16[256,512]{1,0:T(8,128)(2,1)} %get-tuple-element.14.main_ref, bf16[1024,512]{1,0:T(8,128)(2,1)} %get-tuple-element.15.late_ref, bf16[512,4480]{1,0:T(8,128)(2,1)} %bitcast.10, bf16[512,4480]{1,0:T(8,128)(2,1)} %bitcast.11), custom_call_target="tpu_custom_call" | custom-call | tf_op jit(solution)/shard_map/combine/pallas_call | solution.py:296
  209.6 0.0 collective-permute-start
  209.6 3.9 %combine.2 = f32[128,1792]{1,0:T(8,128)} custom-call(s32[1]{0:T(128)} %bitcast.refs_0_.core_ref, bf16[256,512]{1,0:T(8,128)(2,1)} %get-tuple-element.14.main_ref, bf16[1024,512]{1,0:T(8,128)(2,1)} %get-tuple-element.15.late_ref, bf16[512,4480]{1,0:T(8,128)(2,1)} %bitcast.12, bf16[512,4480]{1,0:T(8,128)(2,1)} %bitcast.13), custom_call_target="tpu_custom_call" | custom-call | tf_op jit(solution)/shard_map/combine/pallas_call | solution.py:296
  213.5 0.0 collective-permute-done
  213.5 2.0 add_convert_fusion
Async XLA Ops:
  209.6 3.9 %collective-permute-start = (f32[128,1792]{1,0:T(8,128)}, f32[128,1792]{1,0:T(8,128)S(1)}, u32[]{:S(2)}, u32[]{:S(2)}) collective-permute-start(f32[128,1792]{1,0:T(8,128)} %combine.3), channel_id=1, source_target_pairs={{0,1},{1,0},{2,3},{3,2},{4,5},{5,4},{6,7},{7,6},{8,9},{9,8},{10,11... | collective-permute-start | bytes 2752520 | tf_op jit(solution)/shard_map/ppermute | solution.py:328

commit v4 on v3

v4 whole, which is shorter than its diff:
```python
import jax
import jax.numpy as jnp
from jax import lax
from jax.experimental import pallas as pl
from jax.experimental.pallas import tpu as pltpu
from jax.sharding import PartitionSpec as P

BF16, F32 = jnp.bfloat16, jnp.float32
TILE = 8
LATE = 4
FOLD = TILE // LATE
CORES = ((0, True), (TILE + LATE, False))
BLOCKS = 4
WAIT, HOLD = 65500, 0
TRANSPOSED = (((1,), (1,)), ((), ()))
SMEM_SPEC, VMEM_SPEC, ANY_SPEC = (pl.BlockSpec(memory_space=space) for space in (pltpu.SMEM, pltpu.VMEM, pl.ANY))


def iota(shape, dim):
    return lax.broadcasted_iota(jnp.int32, shape, dim)


def dot(a, b):
    return jnp.dot(a, b, preferred_element_type=F32)


def dot_t(a, b):
    return lax.dot_general(a, b, TRANSPOSED, preferred_element_type=F32)


def spread(experts):
    shape = (experts * TILE, experts)
    return jnp.where(iota(shape, 0) // TILE == iota(shape, 1), 1.0, 0.0).astype(BF16)


def slot_keys(ids_ref, base, experts):
    top, tokens = ids_ref.shape
    number = iota((experts, tokens), 0)
    named = ids_ref[0:1, :] == number
    for k in range(1, top):
        named = named | (ids_ref[k : k + 1, :] == number)
    before = jnp.where(iota((tokens, tokens), 0) < iota((tokens, tokens), 1), 1.0, 0.0).astype(BF16)
    rank = dot(jnp.where(named, 1.0, 0.0).astype(BF16), before)
    key = jnp.where(named, rank - float(base), -100.0).astype(BF16)
    return dot(spread(experts), key)


def main_match(key):
    return key == (iota(key.shape, 0) % TILE).astype(F32)


def late_match(key, q):
    row = iota(key.shape, 0) % TILE
    return (key == (TILE + row % LATE).astype(F32)) & (row // LATE == q)


def dispatch_kernel(experts, base, tail, ids_ref, x_ref, g_ref, out_ref, ready, sems):
    key = slot_keys(ids_ref, base, experts)
    slots, _, width = ready.shape
    main = jnp.where(main_match(key), 1.0, 0.0).astype(BF16)
    if tail:
        late = jnp.concatenate([jnp.where(late_match(key, q), 1.0, 0.0).astype(BF16) for q in range(FOLD)], 1)
    copies = []
    for ref in (x_ref, g_ref):
        parts = [ref[:, b * width : (b + 1) * width] for b in range(BLOCKS)]
        todo = [(main, part) for part in parts]
        if tail:
            per = BLOCKS // FOLD
            todo += [(late, jnp.concatenate(parts[b::per], 0)) for b in range(per)]
        for select, rows in todo:
            n = len(copies)
            if n >= slots:
                copies[n - slots].wait()
            ready[n % slots] = dot(select, rows).astype(BF16)
            copies.append(pltpu.make_async_copy(ready.at[n % slots], out_ref.at[:, n * width : (n + 1) * width], sems.at[n % slots]))
            copies[n].start()
    for copy in copies[-slots:]:
        copy.wait()


def dispatch(ids, x, g, experts, base, tail):
    features = x.shape[1]
    rows, slots = experts * TILE, 4
    columns = features + (features // FOLD if tail else 0)
    return pl.pallas_call(
        lambda *refs: dispatch_kernel(experts, base, tail, *refs),
        in_specs=[VMEM_SPEC] * 3,
        out_specs=ANY_SPEC,
        out_shape=jax.ShapeDtypeStruct((rows, 2 * columns), BF16),
        scratch_shapes=[pltpu.VMEM((slots, rows, features // BLOCKS), BF16), pltpu.SemaphoreType.DMA((slots,))],
        name="dispatch",
    )(ids, x, g)


def weights_kernel(experts, base, tail, nanos, ids_ref, probs_ref, packets_ref, *refs):
    top, tokens = ids_ref.shape
    key = slot_keys(ids_ref, base, experts)
    number = iota((experts, tokens), 0)
    prob = jnp.zeros((experts, tokens), F32)
    for k in range(top):
        prob = prob + jnp.where(ids_ref[k : k + 1, :] == number, probs_ref[k : k + 1, :], 0.0)
    high = prob.astype(BF16)
    low = (prob - high.astype(F32)).astype(BF16)
    for n, part in enumerate((high, low)):
        wide = dot(spread(experts), part)
        refs[1][n * tokens : (n + 1) * tokens, :] = jnp.where(main_match(key), wide, 0.0).T.astype(BF16)
        for q in range(FOLD if tail else 0):
            at = (2 * q + n) * tokens
            refs[2][at : at + tokens, :] = jnp.where(late_match(key, q), wide, 0.0).T.astype(BF16)
    if nanos:
        pl.delay(nanos)


def weights_and_wait(nanos, ids, probs, packets, experts, base, tail):
    tokens, rows = ids.shape[1], experts * TILE
    shapes = [jax.ShapeDtypeStruct((2 * n * tokens, rows), BF16) for n in ((1, FOLD) if tail else (1,))]
    return pl.pallas_call(
        lambda *refs: weights_kernel(experts, base, tail, nanos, *refs),
        in_specs=[VMEM_SPEC] * 2 + [ANY_SPEC],
        out_specs=[ANY_SPEC] + [VMEM_SPEC] * len(shapes),
        out_shape=[jax.ShapeDtypeStruct(packets.shape, packets.dtype)] + shapes,
        input_output_aliases={2: 0},
        name="weights_and_wait",
    )(ids, probs, packets)


def gradients(gate_pre, up_pre, hidden_grad):
    sigmoid = jax.nn.sigmoid(gate_pre)
    common = hidden_grad * sigmoid
    return (common * up_pre * (1.0 + gate_pre * (1.0 - sigmoid))).astype(BF16), (common * gate_pre).astype(BF16)


def unfold_matrix(rows, transposed):
    unfolded, packed = iota((rows, rows), int(transposed)), iota((rows, rows), 1 - int(transposed))
    per = rows // FOLD
    q, rest = unfolded // per, unfolded % per
    at = (rest // LATE) * TILE + LATE * q + rest % LATE
    return jnp.where(at == packed, 1.0, 0.0).astype(BF16)


def start(copies):
    for copy in copies:
        copy.start()


def wait(copies):
    for copy in copies:
        copy.wait()


def expert_kernel(chunks, tail, packet_ref, gate_ref, up_ref, down_ref, out_ref, x_s, g_s, gate_c, up_c, down_c, gate_r, up_r, gg_s, ug_s, in_sems, col_sems, row_sems, tail_s=None, fold_s=None, late_s=None):
    step = pl.program_id(0)
    rows = packet_ref.shape[0]
    wide = out_ref.shape[1]
    width = gate_c.shape[2]
    features = BLOCKS * wide
    folded = features // FOLD
    per = rows // FOLD

    def packet_copies(n, dst):
        at = n * (packet_ref.shape[1] // 2)
        main = pltpu.make_async_copy(packet_ref.at[:, at : at + features], dst.at[0:rows, :], in_sems.at[2 * n])
        if not tail:
            return main, None
        at += features
        return main, pltpu.make_async_copy(packet_ref.at[:, at : at + folded], tail_s.at[n], in_sems.at[2 * n + 1])

    def col_copies(c):
        slot, at = c % 2, pl.multiple_of(c * width, width)
        return (
            pltpu.make_async_copy(gate_ref.at[:, pl.ds(at, width)], gate_c.at[slot], col_sems.at[0, slot]),
            pltpu.make_async_copy(up_ref.at[:, pl.ds(at, width)], up_c.at[slot], col_sems.at[1, slot]),
            pltpu.make_async_copy(down_ref.at[pl.ds(at, width), :], down_c.at[slot], col_sems.at[2, slot]),
        )

    def row_copies(q):
        slot, at = q % 2, pl.multiple_of(q * wide, wide)
        return (
            pltpu.make_async_copy(gate_ref.at[pl.ds(at, wide), :], gate_r.at[slot], row_sems.at[0, slot]),
            pltpu.make_async_copy(up_ref.at[pl.ds(at, wide), :], up_r.at[slot], row_sems.at[1, slot]),
        )

    @pl.when(step == 0)
    def _():
        x_main, x_tail = packet_copies(0, x_s)
        g_main, g_tail = packet_copies(1, g_s)
        gate_0, up_0, down_0 = col_copies(0)
        start([x_tail, x_main, gate_0, up_0, g_tail, g_main, down_0] if tail else [x_main, gate_0, up_0, g_main, down_0])
        start(col_copies(1))
        if tail:
            unfold = unfold_matrix(rows, False)
            fold_s[...] = unfold_matrix(rows, True)

        def unpack(n, dst, copy):
            if tail:
                copy.wait()
                opened = dot(unfold, tail_s[n]).astype(BF16)
                for q in range(FOLD):
                    dst[rows : rows + per, q * folded : (q + 1) * folded] = opened[q * per : (q + 1) * per]

        unpack(0, x_s, x_tail)
        wait((x_main, gate_0))
        gate_pre = dot(x_s[...], gate_c[0])
        up_0.wait()
        up_pre = dot(x_s[...], up_c[0])
        unpack(1, g_s, g_tail)
        wait((g_main, down_0))
        hidden_grad = dot_t(g_s[...], down_c[0])
        gg_s[0], ug_s[0] = gradients(gate_pre, up_pre, hidden_grad)

    @pl.when((step > 0) & (step < chunks))
    def _():
        @pl.when(step < chunks - 1)
        def _():
            start(col_copies(step + 1))

        @pl.when(step == chunks - 1)
        def _():
            start(row_copies(0))
            start(row_copies(1))

        wait(col_copies(step))
        slot = step % 2
        gate_pre = dot(x_s[...], gate_c[slot])
        up_pre = dot(x_s[...], up_c[slot])
        hidden_grad = dot_t(g_s[...], down_c[slot])
        gg_s[step], ug_s[step] = gradients(gate_pre, up_pre, hidden_grad)

    @pl.when((step >= chunks) & (step < chunks + BLOCKS))
    def _():
        q = step - chunks
        slot = q % 2
        wait(row_copies(q))
        gg = jnp.concatenate([gg_s[c] for c in range(chunks)], 1)
        ug = jnp.concatenate([ug_s[c] for c in range(chunks)], 1)
        back = (dot_t(gg, gate_r[slot]) + dot_t(ug, up_r[slot])).astype(BF16)
        out_ref[...] = back[0:rows]
        if tail:
            late_s[q] = back[rows:]

        @pl.when(q < BLOCKS - 2)
        def _():
            start(row_copies(q + 2))

    if tail:

        @pl.when(step >= chunks + BLOCKS)
        def _():
            b = step - chunks - BLOCKS
            stacked = jnp.concatenate([late_s[q * (BLOCKS // FOLD) + b] for q in range(FOLD)], 0)
            out_ref[...] = dot(fold_s[...], stacked).astype(BF16)


def expert_backward(packets, gate, up, down, tail, width):
    features, hidden = gate.shape
    rows = packets.shape[0]
    late = rows // FOLD if tail else 0
    folded = features // FOLD if tail else 0
    wide, chunks = features // BLOCKS, hidden // width
    scratch = [
        pltpu.VMEM((rows + late, features), BF16),
        pltpu.VMEM((rows + late, features), BF16),
        pltpu.VMEM((2, features, width), BF16),
        pltpu.VMEM((2, features, width), BF16),
        pltpu.VMEM((2, width, features), BF16),
        pltpu.VMEM((2, wide, hidden), BF16),
        pltpu.VMEM((2, wide, hidden), BF16),
        pltpu.VMEM((chunks, rows + late, width), BF16),
        pltpu.VMEM((chunks, rows + late, width), BF16),
        pltpu.SemaphoreType.DMA((4,)),
        pltpu.SemaphoreType.DMA((3, 2)),
        pltpu.SemaphoreType.DMA((2, 2)),
    ]
    if tail:
        scratch += [
            pltpu.VMEM((2, rows, folded), BF16),
            pltpu.VMEM((rows, rows), BF16),
            pltpu.VMEM((BLOCKS, late, wide), BF16),
        ]
    return pl.pallas_call(
        lambda *refs: expert_kernel(chunks, tail, *refs),
        grid=(chunks + BLOCKS + folded // wide,),
        in_specs=[ANY_SPEC] * 4,
        out_specs=pl.BlockSpec((rows, wide), lambda s: (0, jnp.maximum(s - chunks, 0))),
        out_shape=jax.ShapeDtypeStruct((rows, features + folded), BF16),
        scratch_shapes=scratch,
        compiler_params=pltpu.CompilerParams(vmem_limit_bytes=60 * 1024 * 1024),
        name="expert_backward",
    )(packets, gate, up, down)


def combine_kernel(main_ref, back_ref, *refs):
    out_ref = refs[-1]
    tokens = out_ref.shape[0]
    both = dot(main_ref[...], back_ref[...])
    if len(refs) > 1:
        both = both + dot(refs[0][...], refs[1][...])
    out_ref[...] = both[:tokens] + both[tokens:]


def combine(half, back, main, late=None):
    rows, tokens = back.shape[0], main.shape[0] // 2
    steps = BLOCKS // 2
    wide = back.shape[1] // (BLOCKS if late is None else BLOCKS + BLOCKS // FOLD)
    in_specs = [pl.BlockSpec(main.shape, lambda s: (0, 0)), pl.BlockSpec((rows, wide), lambda s: (0, steps * half + s))]
    args = [main, back]
    if late is not None:
        in_specs += [pl.BlockSpec((2 * tokens, rows), lambda s: (half, 0)), pl.BlockSpec((rows, wide), lambda s: (0, BLOCKS + s))]
        args += [late, back]
    return pl.pallas_call(
        combine_kernel,
        grid=(steps,),
        in_specs=in_specs,
        out_specs=pl.BlockSpec((tokens, wide), lambda s: (0, s)),
        out_shape=jax.ShapeDtypeStruct((tokens, steps * wide), F32),
        name="combine",
    )(*args)


def exchange(packets, experts):
    parts = packets.reshape(experts, TILE, -1)
    return lax.all_to_all(parts, "ep", split_axis=0, concat_axis=0, tiled=True).reshape(packets.shape)


def share(core, experts, ids, probs, x, g, gate, up, down):
    base, tail = CORES[core]
    packets = dispatch(ids, x, g, experts, base, tail)
    if core == 0:
        arrived, *weights = weights_and_wait(HOLD, ids, probs, exchange(packets, experts), experts, base, tail)
    else:
        packets, *weights = weights_and_wait(WAIT, ids, probs, packets, experts, base, tail)
        arrived = exchange(packets, experts)
    returned = exchange(expert_backward(arrived, gate, up, down, tail, 256), experts)
    return combine(1 - core, returned, *weights), combine(core, returned, *weights)


def body(layer_input, out_grad, expert_ids, gate_probs, gate_proj, up_proj, down_proj):
    experts = lax.axis_size("ep")
    args = (expert_ids.T, gate_probs.T, layer_input, out_grad, gate_proj[0], up_proj[0], down_proj[0])
    paths = [lambda *args, core=core: share(core, experts, *args) for core in (0, 1)]
    crossing, own = lax.cond(lax.axis_index("dp") == 0, *paths, *args)
    return (own + lax.ppermute(crossing, "dp", ((0, 1), (1, 0)))).astype(BF16)


def solution(mesh):
    rows = P("ep", None)
    mats = P("ep", None, None)
    return jax.shard_map(body, mesh=mesh, in_specs=(rows,) * 4 + (mats,) * 3, out_specs=P("ep", "dp"), check_vma=False)
```

time: 216 us -> 205 us (0.949)
  blocking collectives: 107 us -> 94.5 us
  waiting for transfers between devices: 0.01 us -> 2.46 us
    all_to_all x2, blocking collectives: 107 us -> 94.5 us  [exchange(): lax.all_to_all(parts, 'ep', split_axis=0, concat_axis=0, tiled=True)]
    ppermute x1, waiting for transfers between devices: 0.01 us -> 2.46 us  [body(): return (own + lax.ppermute(crossing, 'dp', ((0, 1), (1, 0)))).astype(BF16)]
    pallas_call x6 -> x5, Pallas kernels: 106 us -> 107 us  [the longest x1 66.7 us: weights_and_wait(): pl.pallas_call(lambda *refs: weights_kernel(experts, base, tail, nanos, *...]
  transfers between devices with their start and end apart: 1 -> 1, of which waited for: 0 -> 1; matrix products, arithmetic and copies ran while one was open for 0% -> 0% of each run, Pallas kernels for 2% -> 0%
where the time goes in v4:
time: 205 us
  Pallas kernels  107 us (52%)
  blocking collectives  94.5 us (46%)
  waiting for transfers between devices  2.46 us (1%)
    all_to_all x2, blocking collectives, exchange(): lax.all_to_all(parts, 'ep', split_axis=0, concat_axis=0, tiled=True)  94.5 us
    pallas_call x1, Pallas kernels, weights_and_wait(): pl.pallas_call(lambda *refs: weights_kernel(experts, base, tail, nanos, *...  66.7 us
    pallas_call x1, Pallas kernels, expert_backward(): pl.pallas_call(lambda *refs: expert_kernel(chunks, tail, *refs), grid=(ch...  29.5 us
    pallas_call x1, Pallas kernels, dispatch(): pl.pallas_call(lambda *refs: dispatch_kernel(experts, base, tail, *refs),...  5.91 us
    pallas_call x2, Pallas kernels, combine(): pl.pallas_call(combine_kernel, grid=(steps,), in_specs=in_specs, out_spec...  4.4 us
  transfers between devices with their start and end apart: 1, of which 1 were waited for; matrix products, arithmetic and copies ran while one was open for 0% of the time, Pallas kernels for 0%

profile of v4, /device:TPU:1, one launch (start us, length us, event | category | flops | bytes accessed | tf_op | source)
XLA Modules:
  0.0 204.7 jit_solution(15269138737768099198)
XLA Ops:
  0.0 201.3 %conditional.1 = (f32[128,1792]{1,0:T(8,128)S(1)}, f32[128,1792]{1,0:T(8,128)S(1)}) conditional(s32[]{:T(128)} %convert_element_type.6, (s32[8,128]{1,0:T(8,128)}, bf16[128,3584]{1,0:T(8,128)(2,1)}, bf16[128,3584]{1,0:T(8,128)(2,1)}, f32[8,128]{1,0:T(8,128)}, bf16[3584,1024]{1,0:T(8,128)(2,1)}, /*index=5*/bf16[3584,1024]{1,0:T(8,128)(2,1)}, ...), branch_computations={%region_0.0_spmd, %region_1.0_spmd} | conditional | bytes 33062984 | solution.py:341
  0.0 0.0 copy-start
  0.0 0.0 copy-start.2
  0.0 5.9 %dispatch.2.refs_2_ = bf16[512,7168]{1,0:T(8,128)(2,1)} custom-call(s32[8,128]{1,0:T(8,128)} %get-tuple-element.33.refs_0_, bf16[128,3584]{1,0:T(8,128)(2,1)} %get-tuple-element.35.refs_1_, bf16[128,3584]{1,0:T(8,128)(2,1)} %get-tuple-element.36.refs_2_), custom_call_target="tpu_custom_call" | custom-call | tf_op jit(solution)/shard_map/cond/branch_0_fun/dispatch/pallas_call | solution.py:85
  5.9 0.0 copy-done
  5.9 0.0 copy-done.2
  5.9 66.7 %weights_and_wait.2 = (bf16[512,7168]{1,0:T(8,128)(2,1)}, bf16[256,512]{1,0:T(8,128)(2,1)}) custom-call(s32[8,128]{1,0:T(8,128)S(1)} %copy-done, f32[8,128]{1,0:T(8,128)S(1)} %copy-done.2, bf16[512,7168]{1,0:T(8,128)(2,1)} %dispatch.2.refs_2_), custom_call_target="tpu_custom_call", output_to_operand_aliasing={{0}: (2, {})} | custom-call | tf_op jit(solution)/shard_map/cond/branch_0_fun/weights_and_wait/pallas_call | solution.py:117
  72.7 59.1 %all_to_all.16 = bf16[64,8,7168]{2,1,0:T(8,128)(2,1)} all-to-all(bf16[64,8,7168]{2,1,0:T(8,128)(2,1)} %bitcast.18), channel_id=1, replica_groups=mesh['ep'=64,'dp'=2] {'ep'}, dimensions={0} | all-to-all | bytes 14680064 | tf_op jit(solution)/shard_map/cond/branch_0_fun/all_to_all | solution.py:322
  131.8 29.5 %expert_backward.2 = bf16[512,3584]{1,0:T(8,128)(2,1)} custom-call(bf16[512,7168]{1,0:T(8,128)(2,1)} %bitcast.28, bf16[3584,1024]{1,0:T(8,128)(2,1)} %get-tuple-element.39.refs_1_, bf16[3584,1024]{1,0:T(8,128)(2,1)} %get-tuple-element.40.refs_2_, bf16[1024,3584]{1,0:T(8,128)(2,1)} %get-tuple-element.41.refs_3_), custom_call_target="tpu_custom_call" | custom-call | tf_op jit(solution)/shard_map/cond/branch_0_fun/expert_backward/pallas_call | solution.py:280
  161.3 35.4 %all_to_all.17 = bf16[64,8,3584]{2,1,0:T(8,128)(2,1)} all-to-all(bf16[64,8,3584]{2,1,0:T(8,128)(2,1)} %bitcast.30), channel_id=1, replica_groups=mesh['ep'=64,'dp'=2] {'ep'}, dimensions={0} | all-to-all | bytes 7340032 | tf_op jit(solution)/shard_map/cond/branch_0_fun/all_to_all | solution.py:322
  196.7 2.2 %combine.5 = f32[128,1792]{1,0:T(8,128)S(1)} custom-call(bf16[256,512]{1,0:T(8,128)(2,1)} %get-tuple-element.37.main_ref, bf16[512,3584]{1,0:T(8,128)(2,1)} %bitcast.20), custom_call_target="tpu_custom_call" | custom-call | tf_op jit(solution)/shard_map/cond/branch_0_fun/combine/pallas_call | solution.py:310
  198.9 2.2 %combine.4 = f32[128,1792]{1,0:T(8,128)S(1)} custom-call(bf16[256,512]{1,0:T(8,128)(2,1)} %get-tuple-element.37.main_ref, bf16[512,3584]{1,0:T(8,128)(2,1)} %bitcast.21), custom_call_target="tpu_custom_call" | custom-call | tf_op jit(solution)/shard_map/cond/branch_0_fun/combine/pallas_call | solution.py:310
  201.3 0.1 collective-permute-start
  201.4 2.5 %collective-permute-done = f32[128,1792]{1,0:T(8,128)S(1)} collective-permute-done((f32[128,1792]{1,0:T(8,128)S(1)}, f32[128,1792]{1,0:T(8,128)S(1)}, u32[]{:S(2)}, u32[]{:S(2)}) %collective-permute-start) | collective-permute-done | bytes 917536 | tf_op jit(solution)/shard_map/ppermute | solution.py:342
  203.9 0.9 add_convert_fusion
Async XLA Ops:
  0.0 5.9 %copy-start = (s32[8,128]{1,0:T(8,128)S(1)}, s32[8,128]{1,0:T(8,128)}, u32[]{:S(2)}) copy-start(s32[8,128]{1,0:T(8,128)} %get-tuple-element.33.refs_0_) | copy-start | bytes 12292 | tf_op jit(solution)/shard_map/cond
  0.0 5.9 %copy-start.2 = (f32[8,128]{1,0:T(8,128)S(1)}, f32[8,128]{1,0:T(8,128)}, u32[]{:S(2)}) copy-start(f32[8,128]{1,0:T(8,128)} %get-tuple-element.34.refs_1_) | copy-start | bytes 12292 | tf_op jit(solution)/shard_map/cond
  201.3 2.6 %collective-permute-start = (f32[128,1792]{1,0:T(8,128)S(1)}, f32[128,1792]{1,0:T(8,128)S(1)}, u32[]{:S(2)}, u32[]{:S(2)}) collective-permute-start(f32[128,1792]{1,0:T(8,128)S(1)} %get-tuple-element.55), channel_id=1, source_target_pairs={{0,1},{1,0},{2,3},{3,2},{4,5},{5,4},{6,7},{7,6},{8,9},{9,8},{10,11... | collective-permute-start | bytes 2752520 | tf_op jit(solution)/shard_map/ppermute | solution.py:342

commit v5 on v4

--- a/solution.py
+++ b/solution.py
@@ -11,7 +11,8 @@
 FOLD = TILE // LATE
 CORES = ((0, True), (TILE + LATE, False))
 BLOCKS = 4
-WAIT, HOLD = 65500, 0
+WIDTHS = (512, 256)
+WAIT = 64500
 TRANSPOSED = (((1,), (1,)), ((), ()))
 SMEM_SPEC, VMEM_SPEC, ANY_SPEC = (pl.BlockSpec(memory_space=space) for space in (pltpu.SMEM, pltpu.VMEM, pl.ANY))
 
@@ -153,7 +154,8 @@
     rows = packet_ref.shape[0]
     wide = out_ref.shape[1]
     width = gate_c.shape[2]
-    features = BLOCKS * wide
+    features = x_s.shape[1]
+    blocks = features // wide
     folded = features // FOLD
     per = rows // FOLD
 
@@ -226,7 +228,7 @@
         hidden_grad = dot_t(g_s[...], down_c[slot])
         gg_s[step], ug_s[step] = gradients(gate_pre, up_pre, hidden_grad)
 
-    @pl.when((step >= chunks) & (step < chunks + BLOCKS))
+    @pl.when((step >= chunks) & (step < chunks + blocks))
     def _():
         q = step - chunks
         slot = q % 2
@@ -238,7 +240,7 @@
         if tail:
             late_s[q] = back[rows:]
 
-        @pl.when(q < BLOCKS - 2)
+        @pl.when(q < blocks - 2)
         def _():
             start(row_copies(q + 2))
 
@@ -256,7 +258,8 @@
     rows = packets.shape[0]
     late = rows // FOLD if tail else 0
     folded = features // FOLD if tail else 0
-    wide, chunks = features // BLOCKS, hidden // width
+    blocks = BLOCKS if tail else 7
+    wide, chunks = features // blocks, hidden // width
     scratch = [
         pltpu.VMEM((rows + late, features), BF16),
         pltpu.VMEM((rows + late, features), BF16),
@@ -279,7 +282,7 @@
         ]
     return pl.pallas_call(
         lambda *refs: expert_kernel(chunks, tail, *refs),
-        grid=(chunks + BLOCKS + folded // wide,),
+        grid=(chunks + blocks + folded // wide,),
         in_specs=[ANY_SPEC] * 4,
         out_specs=pl.BlockSpec((rows, wide), lambda s: (0, jnp.maximum(s - chunks, 0))),
         out_shape=jax.ShapeDtypeStruct((rows, features + folded), BF16),
@@ -290,29 +293,45 @@
 
 
 def combine_kernel(main_ref, back_ref, *refs):
-    out_ref = refs[-1]
-    tokens = out_ref.shape[0]
+    step, half = pl.program_id(0), pl.num_programs(0) // 2
+    other_ref, own_ref = refs[-2:]
+    tokens = own_ref.shape[0]
     both = dot(main_ref[...], back_ref[...])
-    if len(refs) > 1:
+    if len(refs) > 2:
         both = both + dot(refs[0][...], refs[1][...])
-    out_ref[...] = both[:tokens] + both[tokens:]
-
-
-def combine(half, back, main, late=None):
+    total = both[:tokens] + both[tokens:]
+
+    @pl.when(step < half)
+    def _():
+        other_ref[...] = total
+
+    @pl.when(step >= half)
+    def _():
+        own_ref[...] = total
+
+
+def combine(core, back, main, late=None):
     rows, tokens = back.shape[0], main.shape[0] // 2
-    steps = BLOCKS // 2
+    half = BLOCKS // 2
     wide = back.shape[1] // (BLOCKS if late is None else BLOCKS + BLOCKS // FOLD)
-    in_specs = [pl.BlockSpec(main.shape, lambda s: (0, 0)), pl.BlockSpec((rows, wide), lambda s: (0, steps * half + s))]
+    block = (lambda s: s) if core else (lambda s: (s + half) % BLOCKS)
+    in_specs = [pl.BlockSpec(main.shape, lambda s: (0, 0)), pl.BlockSpec((rows, wide), lambda s: (0, block(s)))]
     args = [main, back]
     if late is not None:
-        in_specs += [pl.BlockSpec((2 * tokens, rows), lambda s: (half, 0)), pl.BlockSpec((rows, wide), lambda s: (0, BLOCKS + s))]
+        in_specs += [
+            pl.BlockSpec((2 * tokens, rows), lambda s: (block(s) // half, 0)),
+            pl.BlockSpec((rows, wide), lambda s: (0, BLOCKS + s % half)),
+        ]
         args += [late, back]
     return pl.pallas_call(
         combine_kernel,
-        grid=(steps,),
+        grid=(BLOCKS,),
         in_specs=in_specs,
-        out_specs=pl.BlockSpec((tokens, wide), lambda s: (0, s)),
-        out_shape=jax.ShapeDtypeStruct((tokens, steps * wide), F32),
+        out_specs=[
+            pl.BlockSpec((tokens, wide), lambda s: (0, jnp.minimum(s, half - 1))),
+            pl.BlockSpec((tokens, wide), lambda s: (0, jnp.maximum(s - half, 0))),
+        ],
+        out_shape=[jax.ShapeDtypeStruct((tokens, half * wide), F32)] * 2,
         name="combine",
     )(*args)
 
@@ -326,12 +345,14 @@
     base, tail = CORES[core]
     packets = dispatch(ids, x, g, experts, base, tail)
     if core == 0:
-        arrived, *weights = weights_and_wait(HOLD, ids, probs, exchange(packets, experts), experts, base, tail)
+        arrived = exchange(packets, experts)
     else:
         packets, *weights = weights_and_wait(WAIT, ids, probs, packets, experts, base, tail)
         arrived = exchange(packets, experts)
-    returned = exchange(expert_backward(arrived, gate, up, down, tail, 256), experts)
-    return combine(1 - core, returned, *weights), combine(core, returned, *weights)
+    returned = exchange(expert_backward(arrived, gate, up, down, tail, WIDTHS[core]), experts)
+    if core == 0:
+        returned, *weights = weights_and_wait(0, ids, probs, returned, experts, base, tail)
+    return tuple(combine(core, returned, *weights))
 
 
 def body(layer_input, out_grad, expert_ids, gate_probs, gate_proj, up_proj, down_proj):

time: 205 us -> 202 us (0.985)
    pallas_call x2 -> x1, Pallas kernels: 4.4 us -> 4.07 us  [combine(): pl.pallas_call(combine_kernel, grid=(BLOCKS,), in_specs=in_specs, out_spe...]
where the time goes in v5:
time: 202 us
  Pallas kernels  105 us (52%)
  blocking collectives  92.9 us (46%)
  waiting for transfers between devices  2.46 us (1%)
    all_to_all x2, blocking collectives, exchange(): lax.all_to_all(parts, 'ep', split_axis=0, concat_axis=0, tiled=True)  92.9 us
    pallas_call x1, Pallas kernels, weights_and_wait(): pl.pallas_call(lambda *refs: weights_kernel(experts, base, tail, nanos, *...  65.7 us
    pallas_call x1, Pallas kernels, expert_backward(): pl.pallas_call(lambda *refs: expert_kernel(chunks, tail, *refs), grid=(ch...  29.2 us
    pallas_call x1, Pallas kernels, dispatch(): pl.pallas_call(lambda *refs: dispatch_kernel(experts, base, tail, *refs),...  5.95 us
    pallas_call x1, Pallas kernels, combine(): pl.pallas_call(combine_kernel, grid=(BLOCKS,), in_specs=in_specs, out_spe...  4.07 us
  transfers between devices with their start and end apart: 1, of which 1 were waited for; matrix products, arithmetic and copies ran while one was open for 0% of the time, Pallas kernels for 0%

profile of v5, /device:TPU:1, one launch (start us, length us, event | category | flops | bytes accessed | tf_op | source)
XLA Modules:
  0.0 201.5 jit_solution(12690959851450976820)
XLA Ops:
  0.0 198.1 %conditional.1 = ((f32[128,1792]{1,0:T(8,128)S(1)}, f32[128,1792]{1,0:T(8,128)S(1)})) conditional(s32[]{:T(128)} %convert_element_type.6, (s32[8,128]{1,0:T(8,128)}, bf16[128,3584]{1,0:T(8,128)(2,1)}, bf16[128,3584]{1,0:T(8,128)(2,1)}, f32[8,128]{1,0:T(8,128)}, bf16[3584,1024]{1,0:T(8,128)(2,1)}, /*index=5*/bf16[3584,1024]{1,0:T(8,128)(2,1)}, ...), branch_computations={%region_0.0_spmd, %region_1.0_spmd} | conditional | bytes 33062976 | solution.py:362
  0.0 0.0 copy-start
  0.0 0.0 copy-start.2
  0.0 5.9 %dispatch.2.refs_2_ = bf16[512,7168]{1,0:T(8,128)(2,1)} custom-call(s32[8,128]{1,0:T(8,128)} %get-tuple-element.33.refs_0_, bf16[128,3584]{1,0:T(8,128)(2,1)} %get-tuple-element.35.refs_1_, bf16[128,3584]{1,0:T(8,128)(2,1)} %get-tuple-element.36.refs_2_), custom_call_target="tpu_custom_call" | custom-call | tf_op jit(solution)/shard_map/cond/branch_0_fun/dispatch/pallas_call | solution.py:86
  6.0 0.0 copy-done
  6.0 0.0 copy-done.2
  6.0 65.7 %weights_and_wait.2 = (bf16[512,7168]{1,0:T(8,128)(2,1)}, bf16[256,512]{1,0:T(8,128)(2,1)}) custom-call(s32[8,128]{1,0:T(8,128)S(1)} %copy-done, f32[8,128]{1,0:T(8,128)S(1)} %copy-done.2, bf16[512,7168]{1,0:T(8,128)(2,1)} %dispatch.2.refs_2_), custom_call_target="tpu_custom_call", output_to_operand_aliasing={{0}: (2, {})} | custom-call | tf_op jit(solution)/shard_map/cond/branch_0_fun/weights_and_wait/pallas_call | solution.py:118
  71.7 59.1 %all_to_all.16 = bf16[64,8,7168]{2,1,0:T(8,128)(2,1)} all-to-all(bf16[64,8,7168]{2,1,0:T(8,128)(2,1)} %bitcast.14), channel_id=1, replica_groups=mesh['ep'=64,'dp'=2] {'ep'}, dimensions={0} | all-to-all | bytes 14680064 | tf_op jit(solution)/shard_map/cond/branch_0_fun/all_to_all | solution.py:341
  130.8 29.2 %expert_backward.2 = bf16[512,3584]{1,0:T(8,128)(2,1)} custom-call(bf16[512,7168]{1,0:T(8,128)(2,1)} %bitcast.23, bf16[3584,1024]{1,0:T(8,128)(2,1)} %get-tuple-element.39.refs_1_, bf16[3584,1024]{1,0:T(8,128)(2,1)} %get-tuple-element.40.refs_2_, bf16[1024,3584]{1,0:T(8,128)(2,1)} %get-tuple-element.41.refs_3_), custom_call_target="tpu_custom_call" | custom-call | tf_op jit(solution)/shard_map/cond/branch_0_fun/expert_backward/pallas_call | solution.py:283
  160.0 33.8 %all_to_all.17 = bf16[64,8,3584]{2,1,0:T(8,128)(2,1)} all-to-all(bf16[64,8,3584]{2,1,0:T(8,128)(2,1)} %bitcast.26), channel_id=1, replica_groups=mesh['ep'=64,'dp'=2] {'ep'}, dimensions={0} | all-to-all | bytes 7340032 | tf_op jit(solution)/shard_map/cond/branch_0_fun/all_to_all | solution.py:341
  193.8 4.1 %combine.2 = (f32[128,1792]{1,0:T(8,128)S(1)}, f32[128,1792]{1,0:T(8,128)S(1)}) custom-call(bf16[256,512]{1,0:T(8,128)(2,1)} %get-tuple-element.37.main_ref, bf16[512,3584]{1,0:T(8,128)(2,1)} %bitcast.25), custom_call_target="tpu_custom_call" | custom-call | tf_op jit(solution)/shard_map/cond/branch_0_fun/combine/pallas_call | solution.py:326
  198.1 0.1 collective-permute-start
  198.2 2.5 %collective-permute-done = f32[128,1792]{1,0:T(8,128)S(1)} collective-permute-done((f32[128,1792]{1,0:T(8,128)S(1)}, f32[128,1792]{1,0:T(8,128)S(1)}, u32[]{:S(2)}, u32[]{:S(2)}) %collective-permute-start) | collective-permute-done | bytes 917536 | tf_op jit(solution)/shard_map/ppermute | solution.py:363
  200.7 0.9 add_convert_fusion
Async XLA Ops:
  0.0 6.0 %copy-start = (s32[8,128]{1,0:T(8,128)S(1)}, s32[8,128]{1,0:T(8,128)}, u32[]{:S(2)}) copy-start(s32[8,128]{1,0:T(8,128)} %get-tuple-element.33.refs_0_) | copy-start | bytes 12292 | tf_op jit(solution)/shard_map/cond
  0.0 6.0 %copy-start.2 = (f32[8,128]{1,0:T(8,128)S(1)}, f32[8,128]{1,0:T(8,128)}, u32[]{:S(2)}) copy-start(f32[8,128]{1,0:T(8,128)} %get-tuple-element.34.refs_1_) | copy-start | bytes 12292 | tf_op jit(solution)/shard_map/cond
  198.1 2.6 %collective-permute-start = (f32[128,1792]{1,0:T(8,128)S(1)}, f32[128,1792]{1,0:T(8,128)S(1)}, u32[]{:S(2)}, u32[]{:S(2)}) collective-permute-start(f32[128,1792]{1,0:T(8,128)S(1)} %get-tuple-element.55), channel_id=1, source_target_pairs={{0,1},{1,0},{2,3},{3,2},{4,5},{5,4},{6,7},{7,6},{8,9},{9,8},{10,11... | collective-permute-start | bytes 2752520 | tf_op jit(solution)/shard_map/ppermute | solution.py:363

commit v6 on v5

--- a/solution.py
+++ b/solution.py
@@ -303,7 +303,7 @@
 
     @pl.when(step < half)
     def _():
-        other_ref[...] = total
+        other_ref[...] = total.astype(BF16)
 
     @pl.when(step >= half)
     def _():
@@ -331,7 +331,7 @@
             pl.BlockSpec((tokens, wide), lambda s: (0, jnp.minimum(s, half - 1))),
             pl.BlockSpec((tokens, wide), lambda s: (0, jnp.maximum(s - half, 0))),
         ],
-        out_shape=[jax.ShapeDtypeStruct((tokens, half * wide), F32)] * 2,
+        out_shape=[jax.ShapeDtypeStruct((tokens, half * wide), kind) for kind in (BF16, F32)],
         name="combine",
     )(*args)
 
@@ -360,7 +360,7 @@
     args = (expert_ids.T, gate_probs.T, layer_input, out_grad, gate_proj[0], up_proj[0], down_proj[0])
     paths = [lambda *args, core=core: share(core, experts, *args) for core in (0, 1)]
     crossing, own = lax.cond(lax.axis_index("dp") == 0, *paths, *args)
-    return (own + lax.ppermute(crossing, "dp", ((0, 1), (1, 0)))).astype(BF16)
+    return (own + lax.ppermute(crossing, "dp", ((0, 1), (1, 0))).astype(F32)).astype(BF16)
 
 
 def solution(mesh):

time: 202 us -> 201 us (level)
  no operation moved by 1% of the time
where the time goes in v6:
time: 201 us
  Pallas kernels  105 us (52%)
  blocking collectives  92.9 us (46%)
    all_to_all x2, blocking collectives, exchange(): lax.all_to_all(parts, 'ep', split_axis=0, concat_axis=0, tiled=True)  92.9 us
    pallas_call x1, Pallas kernels, weights_and_wait(): pl.pallas_call(lambda *refs: weights_kernel(experts, base, tail, nanos, *...  65.7 us
    pallas_call x1, Pallas kernels, expert_backward(): pl.pallas_call(lambda *refs: expert_kernel(chunks, tail, *refs), grid=(ch...  29.2 us
    pallas_call x1, Pallas kernels, dispatch(): pl.pallas_call(lambda *refs: dispatch_kernel(experts, base, tail, *refs),...  5.95 us
    pallas_call x1, Pallas kernels, combine(): pl.pallas_call(combine_kernel, grid=(BLOCKS,), in_specs=in_specs, out_spe...  4.05 us
  transfers between devices with their start and end apart: 1, of which 1 were waited for; matrix products, arithmetic and copies ran while one was open for 0% of the time, Pallas kernels for 0%

profile of v6, /device:TPU:1, one launch (start us, length us, event | category | flops | bytes accessed | tf_op | source)
XLA Modules:
  0.0 200.8 jit_solution(1377634555310478500)
XLA Ops:
  0.0 198.1 %conditional.1 = ((bf16[128,1792]{1,0:T(8,128)(2,1)S(1)}, f32[128,1792]{1,0:T(8,128)S(1)})) conditional(s32[]{:T(128)} %convert_element_type.9, (s32[8,128]{1,0:T(8,128)}, bf16[128,3584]{1,0:T(8,128)(2,1)}, bf16[128,3584]{1,0:T(8,128)(2,1)}, f32[8,128]{1,0:T(8,128)}, bf16[3584,1024]{1,0:T(8,128)(2,1)}, /*index=5*/bf16[3584,1024]{1,0:T(8,128)(2,1)}, ...), branch_computations={%region_0.0_spmd, %region_1.0_spmd} | conditional | bytes 33062976 | solution.py:362
  0.0 0.0 copy-start
  0.0 0.0 copy-start.2
  0.0 5.9 %dispatch.2.refs_2_ = bf16[512,7168]{1,0:T(8,128)(2,1)} custom-call(s32[8,128]{1,0:T(8,128)} %get-tuple-element.33.refs_0_, bf16[128,3584]{1,0:T(8,128)(2,1)} %get-tuple-element.35.refs_1_, bf16[128,3584]{1,0:T(8,128)(2,1)} %get-tuple-element.36.refs_2_), custom_call_target="tpu_custom_call" | custom-call | tf_op jit(solution)/shard_map/cond/branch_0_fun/dispatch/pallas_call | solution.py:86
  6.0 0.0 copy-done
  6.0 0.0 copy-done.2
  6.0 65.7 %weights_and_wait.2 = (bf16[512,7168]{1,0:T(8,128)(2,1)}, bf16[256,512]{1,0:T(8,128)(2,1)}) custom-call(s32[8,128]{1,0:T(8,128)S(1)} %copy-done, f32[8,128]{1,0:T(8,128)S(1)} %copy-done.2, bf16[512,7168]{1,0:T(8,128)(2,1)} %dispatch.2.refs_2_), custom_call_target="tpu_custom_call", output_to_operand_aliasing={{0}: (2, {})} | custom-call | tf_op jit(solution)/shard_map/cond/branch_0_fun/weights_and_wait/pallas_call | solution.py:118
  71.7 59.1 %all_to_all.16 = bf16[64,8,7168]{2,1,0:T(8,128)(2,1)} all-to-all(bf16[64,8,7168]{2,1,0:T(8,128)(2,1)} %bitcast.14), channel_id=1, replica_groups=mesh['ep'=64,'dp'=2] {'ep'}, dimensions={0} | all-to-all | bytes 14680064 | tf_op jit(solution)/shard_map/cond/branch_0_fun/all_to_all | solution.py:341
  130.8 29.2 %expert_backward.2 = bf16[512,3584]{1,0:T(8,128)(2,1)} custom-call(bf16[512,7168]{1,0:T(8,128)(2,1)} %bitcast.23, bf16[3584,1024]{1,0:T(8,128)(2,1)} %get-tuple-element.39.refs_1_, bf16[3584,1024]{1,0:T(8,128)(2,1)} %get-tuple-element.40.refs_2_, bf16[1024,3584]{1,0:T(8,128)(2,1)} %get-tuple-element.41.refs_3_), custom_call_target="tpu_custom_call" | custom-call | tf_op jit(solution)/shard_map/cond/branch_0_fun/expert_backward/pallas_call | solution.py:283
  160.0 33.8 %all_to_all.17 = bf16[64,8,3584]{2,1,0:T(8,128)(2,1)} all-to-all(bf16[64,8,3584]{2,1,0:T(8,128)(2,1)} %bitcast.26), channel_id=1, replica_groups=mesh['ep'=64,'dp'=2] {'ep'}, dimensions={0} | all-to-all | bytes 7340032 | tf_op jit(solution)/shard_map/cond/branch_0_fun/all_to_all | solution.py:341
  193.8 4.0 %combine.2 = (bf16[128,1792]{1,0:T(8,128)(2,1)S(1)}, f32[128,1792]{1,0:T(8,128)S(1)}) custom-call(bf16[256,512]{1,0:T(8,128)(2,1)} %get-tuple-element.37.main_ref, bf16[512,3584]{1,0:T(8,128)(2,1)} %bitcast.25), custom_call_target="tpu_custom_call" | custom-call | tf_op jit(solution)/shard_map/cond/branch_0_fun/combine/pallas_call | solution.py:326
  198.1 0.1 collective-permute-start
  198.2 1.8 collective-permute-done
  200.0 0.8 add_convert_fusion
Async XLA Ops:
  0.0 6.0 %copy-start = (s32[8,128]{1,0:T(8,128)S(1)}, s32[8,128]{1,0:T(8,128)}, u32[]{:S(2)}) copy-start(s32[8,128]{1,0:T(8,128)} %get-tuple-element.33.refs_0_) | copy-start | bytes 12292 | tf_op jit(solution)/shard_map/cond
  0.0 6.0 %copy-start.2 = (f32[8,128]{1,0:T(8,128)S(1)}, f32[8,128]{1,0:T(8,128)}, u32[]{:S(2)}) copy-start(f32[8,128]{1,0:T(8,128)} %get-tuple-element.34.refs_1_) | copy-start | bytes 12292 | tf_op jit(solution)/shard_map/cond
  198.1 1.9 collective-permute-start
